TPU v7x, 32 devices: a whole 2x2x4 slice. The times are simulated.
32 devices in a mesh: rep: 8 (over y, x, core), tp: 4 (over z).
Axes of the slice: x: 2, y: 2, z: 4, core: 2. Of those that a mesh axis runs over, the one named last changes fastest.
Arguments:
- flat_buffer: bfloat16 [578912256], P(('rep', 'tp')), may hold values from -60 to 60
- shard_pad: int32 [2, 6], replicated, may hold values from 0 to 2
Outputs:
- q_served: bfloat16 [2, 6144, 6144], P(None, 'rep', 'tp')
- q_scale: float32 [2, 48, 6144], P(None, 'rep', 'tp')
- k_served: bfloat16 [2, 6144, 1024], P(None, 'rep', 'tp')
- k_scale: float32 [2, 48, 1024], P(None, 'rep', 'tp')
- v_served: bfloat16 [2, 6144, 1024], P(None, 'rep', 'tp')
- v_scale: float32 [2, 48, 1024], P(None, 'rep', 'tp')
- o_served: bfloat16 [2, 6144, 6144], P(None, 'tp', 'rep')
- o_scale: float32 [2, 48, 6144], P(None, 'tp', 'rep')
- gate_served: bfloat16 [2, 6144, 16384], P(None, 'rep', 'tp')
- gate_scale: float32 [2, 48, 16384], P(None, 'rep', 'tp')
- up_served: bfloat16 [2, 6144, 16384], P(None, 'rep', 'tp')
- up_scale: float32 [2, 48, 16384], P(None, 'rep', 'tp')
All inputs are finite; a program needn't handle non-finite values. Where the computation divides by a largest or mean magnitude, that divisor is 1e-20 or more.
Results may differ from a plain program's by a relative error of at most 0.001.
Values may be sent and summed in bfloat16 or wider, within the bound.
A program may use at most 192 MiB of HBM per device.

v0:
```python
import functools

import jax
import jax.numpy as jnp
from jax import lax
from jax.experimental import pallas as pl
from jax.experimental.pallas import tpu as pltpu
from jax.sharding import PartitionSpec as P

D = 6144
KV = 1024
FF = 16384
GROUP = 128
LAYERS = 2


def quantize_kernel(order, *refs):
    received, scaled, scale = refs[0], refs[-2], refs[-1]
    group = pl.program_id(0)
    parts = [received[where + (0,)].astype(jnp.float32) for where in order]
    served = jnp.concatenate(parts, axis=0).T
    peak = jnp.max(jnp.abs(served), axis=0, keepdims=True) + 1e-06
    scaled[0] = (served / peak).astype(jnp.bfloat16)
    scale[0, pl.ds(group, 1), :] = peak


def quantize(received, layer, earlier):
    lead = received.shape[:-3]
    groups, rows, width = received.shape[-3:]
    if len(lead) == 2:
        order = [(inner, outer) for outer in range(lead[1]) for inner in range(lead[0])]
    else:
        order = [(inner,) for inner in range(lead[0])]
    total = len(order) * rows
    block = lead + (1, rows, width)
    zeros = (0,) * len(lead)
    return pl.pallas_call(
        functools.partial(quantize_kernel, order),
        grid=(groups,),
        in_specs=[pl.BlockSpec(block, lambda g: zeros + (g, 0, 0))]
        + [pl.BlockSpec(memory_space=pl.ANY)] * len(earlier),
        out_specs=[
            pl.BlockSpec((1, GROUP, total), lambda g: (layer, g, 0)),
            pl.BlockSpec((1, groups, total), lambda g: (layer, 0, 0)),
        ],
        out_shape=[
            jax.ShapeDtypeStruct((LAYERS, groups * GROUP, total), jnp.bfloat16),
            jax.ShapeDtypeStruct((LAYERS, groups, total), jnp.float32),
        ],
        input_output_aliases={1 + i: i for i in range(len(earlier))},
        cost_estimate=pl.CostEstimate(
            flops=20 * groups * GROUP * total,
            bytes_accessed=4 * groups * GROUP * total,
            transcendentals=0,
        ),
    )(received, *earlier)


def on_device(flat_buffer, shard_pad):
    reps = lax.axis_size("rep")
    tps = lax.axis_size("tp")
    devices = reps * tps
    widths = (D, KV, KV, D, FF, FF)
    tiled = flat_buffer.reshape(flat_buffer.shape[0] // GROUP, GROUP)
    offsets = []
    offset = jnp.zeros((), jnp.int32)
    for layer in range(LAYERS):
        for index in range(6):
            offsets.append(offset)
            offset = offset + widths[index] // devices * D // GROUP + shard_pad[layer, index]
    outputs = [()] * 6
    for layer in range(LAYERS):
        for index in (4, 5, 0, 3, 1, 2):
            rows = widths[index] // devices
            lines = D // GROUP
            taken = lax.dynamic_slice_in_dim(tiled, offsets[layer * 6 + index], rows * lines, 0)
            piece = taken.reshape(rows, lines, GROUP).transpose(1, 0, 2)
            if index == 3:
                received = lax.all_to_all(piece, "tp", split_axis=0, concat_axis=0, tiled=True)
                received = received.reshape(tps, lines // tps, rows, GROUP)
            else:
                received = lax.all_to_all(piece, "rep", split_axis=0, concat_axis=0, tiled=True)
                received = received.reshape(reps, lines // reps, rows, GROUP)
                received = lax.all_to_all(received, "tp", split_axis=0, concat_axis=0, tiled=True)
                received = received.reshape(tps, reps // tps, lines // reps, rows, GROUP)
            outputs[index] = quantize(received, layer, tuple(outputs[index]))
    return tuple(array for pair in outputs for array in pair)


def solution(mesh):
    column = P(None, "rep", "tp")
    row = P(None, "tp", "rep")
    return jax.shard_map(
        on_device,
        mesh=mesh,
        in_specs=(P(("rep", "tp")), P()),
        out_specs=(column,) * 6 + (row,) * 2 + (column,) * 4,
        check_vma=False,
    )
```

profile of v0, /device:TPU:1, one launch (start us, length us, event | category | flops | bytes accessed | tf_op | source)
XLA Modules:
  0.0 1302.1 jit_solution(7797727800659231753)
XLA Ops:
  0.6 1.7 fusion
  8.9 1.8 constant_dynamic-slice_fusion.6
  11.5 5.2 all-to-all-start.6
  17.6 5.5 all-to-all-done.6
  23.1 5.3 all-to-all-start.4
  29.2 5.6 all-to-all-done.4
  34.8 5.9 all-to-all-start.10
  40.8 6.4 all-to-all-done.10
  47.2 12.3 all_to_all.110
  59.6 14.8 %all_to_all.111 = bf16[8,6,32,128]{3,2,1,0:T(8,128)(2,1)} all-to-all(bf16[8,6,32,128]{3,2,1,0:T(8,128)(2,1)S(1)} %bitcast.93), channel_id=1, replica_groups=mesh['rep'=8,'tp'=4] {'tp'}, dimensions={0} | all-to-all | bytes 786432 | tf_op jit(solution)/shard_map/all_to_all | solution.py:84
  74.4 13.9 %all_to_all.112 = bf16[8,6,32,128]{3,2,1,0:T(8,128)(2,1)} all-to-all(bf16[8,6,32,128]{3,2,1,0:T(8,128)(2,1)S(1)} %bitcast.94), channel_id=1, replica_groups=mesh['rep'=8,'tp'=4] {'tp'}, dimensions={0} | all-to-all | bytes 786432 | tf_op jit(solution)/shard_map/all_to_all | solution.py:84
  88.3 3.5 all-to-all-start.11
  92.4 8.6 all-to-all-done.11
  101.0 4.1 all-to-all-start.9
  105.1 5.4 constant_dynamic-slice_fusion.4
  110.5 2.0 copy.68
  112.5 1.6 all-to-all-done.9
  114.1 7.1 all-to-all-start
  121.3 1.7 dynamic_slice.37
  123.0 2.0 copy.69
  125.0 22.2 %all-to-all-done = bf16[48,192,128]{2,1,0:T(8,128)(2,1)S(1)} async-done(((bf16[48,192,128]{2,1,0:T(8,128)(2,1)}), bf16[48,192,128]{2,1,0:T(8,128)(2,1)S(1)}, u32[]{:S(2)}, u32[]{:S(2)}) %all-to-all-start) | async-done | bytes 2359328 | tf_op jit(solution)/shard_map/all_to_all | solution.py:82
  147.2 7.8 all-to-all-start.2
  155.0 3.7 copy.75
  158.6 22.3 %all-to-all-done.2 = bf16[48,192,128]{2,1,0:T(8,128)(2,1)} async-done(((bf16[48,192,128]{2,1,0:T(8,128)(2,1)}), bf16[48,192,128]{2,1,0:T(8,128)(2,1)}, u32[]{:S(2)}, u32[]{:S(2)}) %all-to-all-start.2) | async-done | bytes 2359328 | tf_op jit(solution)/shard_map/all_to_all | solution.py:82
  180.9 3.6 all-to-all-start.13
  184.6 3.7 copy.74
  188.2 49.7 %all-to-all-done.13 = bf16[48,192,128]{2,1,0:T(8,128)(2,1)S(1)} async-done(((bf16[48,192,128]{2,1,0:T(8,128)(2,1)}), bf16[48,192,128]{2,1,0:T(8,128)(2,1)S(1)}, u32[]{:S(2)}, u32[]{:S(2)}) %all-to-all-start.13) | async-done | bytes 2359328 | tf_op jit(solution)/shard_map/all_to_all | solution.py:79
  239.3 3.6 all-to-all-start.12
  244.2 17.2 %constant_dynamic-slice_fusion = (bf16[24576,128]{1,0:T(8,128)(2,1)S(1)}, bf16[24576,128]{1,0:T(8,128)(2,1)}, bf16[24576,128]{1,0:T(8,128)(2,1)}, bf16[24576,128]{1,0:T(8,128)(2,1)}) fusion(bf16[141336,128]{1,0:T(8,128)(2,1)} %bitcast.73, s32[]{:T(128)S(6)} %select_n.43, s32[]{:T(128)S(6)} %select_n.42, s32[]{:T(128)S(6)} %select_n.41, s32[]{:T(128)S(6)} %select_n.40), kind=kLoop, calls=%fused_computation | loop fusion | bytes 50331664 | tf_op jit(solution)/shard_map/dynamic_slice | solution.py:76
  261.4 4.2 copy.79
  265.6 30.6 %all-to-all-done.12 = bf16[48,192,128]{2,1,0:T(8,128)(2,1)S(1)} async-done(((bf16[48,192,128]{2,1,0:T(8,128)(2,1)}), bf16[48,192,128]{2,1,0:T(8,128)(2,1)S(1)}, u32[]{:S(2)}, u32[]{:S(2)}) %all-to-all-start.12) | async-done | bytes 2359328 | tf_op jit(solution)/shard_map/all_to_all | solution.py:79
  297.7 6.4 all-to-all-start.20
  304.1 7.1 copy.78
  311.2 61.0 %all-to-all-done.20 = bf16[48,512,128]{2,1,0:T(8,128)(2,1)} async-done(((bf16[48,512,128]{2,1,0:T(8,128)(2,1)}), bf16[48,512,128]{2,1,0:T(8,128)(2,1)}, u32[]{:S(2)}, u32[]{:S(2)}) %all-to-all-start.20) | async-done | bytes 6291488 | tf_op jit(solution)/shard_map/all_to_all | solution.py:82
  372.2 8.1 all-to-all-start.18
  380.4 7.1 copy.77
  387.4 61.0 %all-to-all-done.18 = bf16[48,512,128]{2,1,0:T(8,128)(2,1)} async-done(((bf16[48,512,128]{2,1,0:T(8,128)(2,1)}), bf16[48,512,128]{2,1,0:T(8,128)(2,1)}, u32[]{:S(2)}, u32[]{:S(2)}) %all-to-all-start.18) | async-done | bytes 6291488 | tf_op jit(solution)/shard_map/all_to_all | solution.py:82
  448.5 8.2 all-to-all-start.16
  456.7 7.1 copy.76
  463.8 61.0 %all-to-all-done.16 = bf16[48,512,128]{2,1,0:T(8,128)(2,1)} async-done(((bf16[48,512,128]{2,1,0:T(8,128)(2,1)}), bf16[48,512,128]{2,1,0:T(8,128)(2,1)}, u32[]{:S(2)}, u32[]{:S(2)}) %all-to-all-start.16) | async-done | bytes 6291488 | tf_op jit(solution)/shard_map/all_to_all | solution.py:82
  524.8 79.2 %all_to_all.113 = bf16[48,512,128]{2,1,0:T(8,128)(2,1)} all-to-all(bf16[48,512,128]{2,1,0:T(8,128)(2,1)} %copy.76), channel_id=1, replica_groups=mesh['rep'=8,'tp'=4] {'rep'}, dimensions={0} | all-to-all | bytes 12582912 | tf_op jit(solution)/shard_map/all_to_all | solution.py:82
  604.1 56.1 %all_to_all.114 = bf16[8,6,192,128]{3,2,1,0:T(8,128)(2,1)} all-to-all(bf16[8,6,192,128]{3,2,1,0:T(8,128)(2,1)S(1)} %bitcast.85), channel_id=1, replica_groups=mesh['rep'=8,'tp'=4] {'tp'}, dimensions={0} | all-to-all | bytes 4718592 | tf_op jit(solution)/shard_map/all_to_all | solution.py:84
  660.1 57.4 %all_to_all.115 = bf16[8,6,192,128]{3,2,1,0:T(8,128)(2,1)} all-to-all(bf16[8,6,192,128]{3,2,1,0:T(8,128)(2,1)} %bitcast.12), channel_id=1, replica_groups=mesh['rep'=8,'tp'=4] {'tp'}, dimensions={0} | all-to-all | bytes 4718592 | tf_op jit(solution)/shard_map/all_to_all | solution.py:84
  717.5 143.8 %all_to_all.116 = bf16[8,6,512,128]{3,2,1,0:T(8,128)(2,1)} all-to-all(bf16[8,6,512,128]{3,2,1,0:T(8,128)(2,1)} %bitcast.57), channel_id=1, replica_groups=mesh['rep'=8,'tp'=4] {'tp'}, dimensions={0} | all-to-all | bytes 12582912 | tf_op jit(solution)/shard_map/all_to_all | solution.py:84
  861.3 143.9 %all_to_all.117 = bf16[8,6,512,128]{3,2,1,0:T(8,128)(2,1)} all-to-all(bf16[8,6,512,128]{3,2,1,0:T(8,128)(2,1)} %bitcast.53), channel_id=1, replica_groups=mesh['rep'=8,'tp'=4] {'tp'}, dimensions={0} | all-to-all | bytes 12582912 | tf_op jit(solution)/shard_map/all_to_all | solution.py:84
  1005.2 143.8 %all_to_all.118 = bf16[8,6,512,128]{3,2,1,0:T(8,128)(2,1)} all-to-all(bf16[8,6,512,128]{3,2,1,0:T(8,128)(2,1)} %bitcast.48), channel_id=1, replica_groups=mesh['rep'=8,'tp'=4] {'tp'}, dimensions={0} | all-to-all | bytes 12582912 | tf_op jit(solution)/shard_map/all_to_all | solution.py:84
  1149.0 5.3 all-to-all-start.15
  1154.3 4.2 shard_map.123
  1158.5 4.2 shard_map.124
  1164.0 4.2 shard_map.125
  1168.2 4.2 shard_map.126
  1173.8 8.4 shard_map.127
  1182.2 8.4 shard_map.128
  1190.6 1.6 copy.83
  1192.2 5.4 shard_map.121
  1197.5 5.4 shard_map.122
  1202.9 1.6 copy.80
  1204.5 8.3 shard_map.131
  1212.8 8.3 shard_map.132
  1221.1 1.8 copy.85
  1222.9 8.3 shard_map.129
  1231.2 60.7 %all-to-all-done.15 = bf16[8,6,512,128]{3,2,1,0:T(8,128)(2,1)} async-done(((bf16[8,6,512,128]{3,2,1,0:T(8,128)(2,1)}), bf16[8,6,512,128]{3,2,1,0:T(8,128)(2,1)}, u32[]{:S(2)}, u32[]{:S(2)}) %all-to-all-start.15) | async-done | bytes 6291488 | tf_op jit(solution)/shard_map/all_to_all | solution.py:84
  1292.0 8.3 shard_map.130
  1300.3 1.8 copy.84
  (18 shorter events, 8.1 us)
Async XLA Ops:
  11.5 11.6 all-to-all-start.6
  23.1 11.7 all-to-all-start.4
  34.8 12.4 all-to-all-start.10
  88.3 12.7 all-to-all-start.11
  101.0 9.5 copy-start.4
  101.0 13.1 %all-to-all-start.9 = ((bf16[8,6,32,128]{3,2,1,0:T(8,128)(2,1)}), bf16[8,6,32,128]{3,2,1,0:T(8,128)(2,1)S(1)}, u32[]{:S(2)}, u32[]{:S(2)}) async-start(bf16[8,6,32,128]{3,2,1,0:T(8,128)(2,1)} %bitcast.28), calls=%async_computation.9 | async-start | bytes 786432 | tf_op jit(solution)/shard_map/all_to_all | solution.py:84
  114.1 10.9 copy-start.5
  114.1 33.1 %all-to-all-start = ((bf16[48,192,128]{2,1,0:T(8,128)(2,1)}), bf16[48,192,128]{2,1,0:T(8,128)(2,1)S(1)}, u32[]{:S(2)}, u32[]{:S(2)}) async-start(bf16[48,192,128]{2,1,0:T(8,128)(2,1)} %copy.68), calls=%async_computation | async-start | bytes 4718592 | tf_op jit(solution)/shard_map/all_to_all | solution.py:82
  147.2 33.7 %copy-start.2 = (bf16[48,192,128]{2,1,0:T(8,128)(2,1)}, bf16[48,192,128]{2,1,0:T(8,128)(2,1)S(1)}, u32[]{:S(2)}) copy-start(bf16[48,192,128]{2,1,0:T(8,128)(2,1)S(1)} %all-to-all-done) | copy-start | bytes 7077892
  147.2 33.7 %all-to-all-start.2 = ((bf16[48,192,128]{2,1,0:T(8,128)(2,1)}), bf16[48,192,128]{2,1,0:T(8,128)(2,1)}, u32[]{:S(2)}, u32[]{:S(2)}) async-start(bf16[48,192,128]{2,1,0:T(8,128)(2,1)} %copy.69), calls=%async_computation.2 | async-start | bytes 4718592 | tf_op jit(solution)/shard_map/all_to_all | solution.py:82
  180.9 57.0 %all-to-all-start.13 = ((bf16[48,192,128]{2,1,0:T(8,128)(2,1)}), bf16[48,192,128]{2,1,0:T(8,128)(2,1)S(1)}, u32[]{:S(2)}, u32[]{:S(2)}) async-start(bf16[48,192,128]{2,1,0:T(8,128)(2,1)} %copy.75), calls=%async_computation.13 | async-start | bytes 4718592 | tf_op jit(solution)/shard_map/all_to_all | solution.py:79
  237.9 1.4 copy-start.1
  239.3 57.0 %all-to-all-start.12 = ((bf16[48,192,128]{2,1,0:T(8,128)(2,1)}), bf16[48,192,128]{2,1,0:T(8,128)(2,1)S(1)}, u32[]{:S(2)}, u32[]{:S(2)}) async-start(bf16[48,192,128]{2,1,0:T(8,128)(2,1)} %copy.74), calls=%async_computation.12 | async-start | bytes 4718592 | tf_op jit(solution)/shard_map/all_to_all | solution.py:79
  296.3 1.4 copy-start
  297.7 74.6 %all-to-all-start.20 = ((bf16[48,512,128]{2,1,0:T(8,128)(2,1)}), bf16[48,512,128]{2,1,0:T(8,128)(2,1)}, u32[]{:S(2)}, u32[]{:S(2)}) async-start(bf16[48,512,128]{2,1,0:T(8,128)(2,1)} %copy.79), calls=%async_computation.20 | async-start | bytes 12582912 | tf_op jit(solution)/shard_map/all_to_all | solution.py:82
  372.2 76.2 %all-to-all-start.18 = ((bf16[48,512,128]{2,1,0:T(8,128)(2,1)}), bf16[48,512,128]{2,1,0:T(8,128)(2,1)}, u32[]{:S(2)}, u32[]{:S(2)}) async-start(bf16[48,512,128]{2,1,0:T(8,128)(2,1)} %copy.78), calls=%async_computation.18 | async-start | bytes 12582912 | tf_op jit(solution)/shard_map/all_to_all | solution.py:82
  448.5 76.3 %all-to-all-start.16 = ((bf16[48,512,128]{2,1,0:T(8,128)(2,1)}), bf16[48,512,128]{2,1,0:T(8,128)(2,1)}, u32[]{:S(2)}, u32[]{:S(2)}) async-start(bf16[48,512,128]{2,1,0:T(8,128)(2,1)} %copy.77), calls=%async_computation.16 | async-start | bytes 12582912 | tf_op jit(solution)/shard_map/all_to_all | solution.py:82
  463.8 140.2 %copy-start.3 = (bf16[48,192,128]{2,1,0:T(8,128)(2,1)S(1)}, bf16[48,192,128]{2,1,0:T(8,128)(2,1)}, u32[]{:S(2)}) copy-start(bf16[48,192,128]{2,1,0:T(8,128)(2,1)} %copy-done.2) | copy-start | bytes 7077892
  1149.0 143.0 %all-to-all-start.15 = ((bf16[8,6,512,128]{3,2,1,0:T(8,128)(2,1)}), bf16[8,6,512,128]{3,2,1,0:T(8,128)(2,1)}, u32[]{:S(2)}, u32[]{:S(2)}) async-start(bf16[8,6,512,128]{3,2,1,0:T(8,128)(2,1)} %bitcast.74), calls=%async_computation.15 | async-start | bytes 12582912 | tf_op jit(solution)/shard_map/all_to_all | solution.py:84
where the time goes:
time: 1310 us; the launch traced here: 1300 us
  blocking collectives  665 us (51%)
  waiting for transfers between devices  396 us (30%)
  local copies, waits for them, and re-layouts  79.5 us (6%)
  Pallas kernels  77.7 us (6%)
  starting transfers between devices  74.2 us (6%)
    all_to_all x7, blocking collectives, on_device(): lax.all_to_all(received, 'tp', split_axis=0, concat_axis=0, tiled=True)  574 us
    all_to_all x8, waiting for transfers between devices, on_device(): lax.all_to_all(piece, 'rep', split_axis=0, concat_axis=0, tiled=True)  245 us
    all_to_all x2, blocking collectives, on_device(): lax.all_to_all(piece, 'rep', split_axis=0, concat_axis=0, tiled=True)  91.6 us
    all_to_all x2, waiting for transfers between devices, on_device(): lax.all_to_all(piece, 'tp', split_axis=0, concat_axis=0, tiled=True)  80.3 us
    pallas_call x12, Pallas kernels, quantize(): pl.pallas_call(functools.partial(quantize_kernel, order), grid=(groups,),...  77.7 us
    all_to_all x3, waiting for transfers between devices, on_device(): lax.all_to_all(received, 'tp', split_axis=0, concat_axis=0, tiled=True)  70.9 us
    all_to_all x8, starting transfers between devices, on_device(): lax.all_to_all(piece, 'rep', split_axis=0, concat_axis=0, tiled=True)  54.1 us
    transpose x12, local copies, waits for them, and re-layouts, on_device(): piece = taken.reshape(rows, lines, GROUP).transpose(1, 0, 2)  39.5 us
  transfers between devices with their start and end apart: 13, of which 13 were waited for; matrix products, arithmetic and copies ran while one was open for 5% of the time, Pallas kernels for 5%

commit v1 on v0

v1 whole, which is shorter than its diff:
```python
import functools
import math

import jax
import jax.numpy as jnp
import numpy as np
from jax import lax
from jax.experimental import pallas as pl
from jax.experimental.pallas import tpu as pltpu
from jax.sharding import PartitionSpec as P

D = 6144
KV = 1024
FF = 16384
GROUP = 128
LAYERS = 2
WIDTHS = (D, KV, KV, D, FF, FF)
LINES = D // GROUP
ORDER = [(index, layer) for index in (0, 1, 2, 4, 5) for layer in range(LAYERS)]
CHUNKS = 16
AHEAD = 2


def prepare_kernel(starts, window, out, wide):
    rows = out.shape[1]
    shift = starts[pl.program_id(0)] % 8
    wide[...] = window[...].astype(jnp.float32)
    for line in range(LINES):
        picked = wide[pl.ds(shift + line, rows, stride=LINES), :]
        out[line] = picked.astype(jnp.bfloat16)


def prepare(tiled, starts, rows):
    steps = starts.shape[0]
    span = rows * LINES + 8
    return pl.pallas_call(
        prepare_kernel,
        grid_spec=pltpu.PrefetchScalarGridSpec(
            num_scalar_prefetch=1,
            grid=(steps,),
            in_specs=[
                pl.BlockSpec(
                    (pl.Element(span), pl.Element(GROUP)),
                    lambda i, starts: (pl.multiple_of(starts[i] // 8 * 8, 8), 0),
                )
            ],
            out_specs=pl.BlockSpec((LINES, rows, GROUP), lambda i, starts: (0, i, 0)),
            scratch_shapes=[pltpu.VMEM((span, GROUP), jnp.float32)],
        ),
        out_shape=jax.ShapeDtypeStruct((LINES, steps * rows, GROUP), jnp.bfloat16),
        cost_estimate=pl.CostEstimate(
            flops=4 * steps * span * GROUP,
            bytes_accessed=4 * steps * span * GROUP,
            transcendentals=0,
        ),
    )(starts, tiled)


def exchange_kernel(reps, tps, sent, arrived, passing, send_a, recv_a, send_b, recv_b, kept):
    rep = lax.axis_index("rep")
    tp = lax.axis_index("tp")
    ratio = reps // tps
    depth = LINES // reps
    rows = sent.shape[1] // CHUNKS
    target = rep // ratio

    def at(device_rep, device_tp):
        return dict(
            device_id=(device_rep, device_tp), device_id_type=pl.DeviceIdType.MESH
        )

    barrier = pltpu.get_barrier_semaphore()
    for hop in range(1, reps):
        pl.semaphore_signal(barrier, inc=1, **at((rep + hop) % reps, tp))
    for hop in range(1, tps):
        pl.semaphore_signal(barrier, inc=1, **at(rep, (tp + hop) % tps))
    pl.semaphore_wait(barrier, reps + tps - 2)

    def block(chunk):
        return pl.ds(pl.multiple_of(chunk * rows, 8), rows)

    def mine(chunk, owner):
        return sent.at[pl.ds(owner * depth, depth), block(chunk)]

    def spread(chunk):
        for hop in range(1, reps):
            owner = (rep + hop) % reps

            def go(place):
                pltpu.make_async_remote_copy(
                    src_ref=mine(chunk, owner),
                    dst_ref=place,
                    send_sem=send_a.at[chunk],
                    recv_sem=recv_a.at[chunk],
                    **at(owner, tp),
                ).start()

            @pl.when(target == tp)
            def _():
                go(arrived.at[tp, rep % ratio, :, block(chunk)])

            @pl.when(target != tp)
            def _():
                go(passing.at[rep, :, block(chunk)])

    def forward(chunk):
        for hop in range(1, tps):
            there = (tp + hop) % tps
            for part in range(ratio):
                source = there * ratio + part

                def go(data):
                    pltpu.make_async_remote_copy(
                        src_ref=data,
                        dst_ref=arrived.at[tp, part, :, block(chunk)],
                        send_sem=send_b.at[chunk],
                        recv_sem=recv_b.at[chunk],
                        **at(rep, there),
                    ).start()

                @pl.when(source == rep)
                def _():
                    go(mine(chunk, rep))

                @pl.when(source != rep)
                def _():
                    go(passing.at[source, :, block(chunk)])

    @pl.when(target == tp)
    def _():
        pltpu.make_async_copy(
            sent.at[pl.ds(rep * depth, depth)], arrived.at[tp, rep % ratio], kept
        ).start()

    for chunk in range(AHEAD):
        spread(chunk)

    def wait(semaphore, chunk, count):
        whole = passing.at[pl.ds(0, count), :, block(chunk)]
        pltpu.make_async_copy(whole, whole, semaphore.at[chunk]).wait()

    @pl.loop(0, CHUNKS)
    def _(chunk):
        @pl.when(chunk + AHEAD < CHUNKS)
        def _():
            spread(chunk + AHEAD)

        wait(recv_a, chunk, reps - 1)
        forward(chunk)

    @pl.loop(0, CHUNKS)
    def _(chunk):
        wait(send_a, chunk, reps - 1)
        wait(send_b, chunk, ratio * (tps - 1))
        wait(recv_b, chunk, ratio * (tps - 1))

    @pl.when(target == tp)
    def _():
        pltpu.make_async_copy(
            sent.at[pl.ds(rep * depth, depth)], arrived.at[tp, rep % ratio], kept
        ).wait()


def exchange(sent, reps, tps):
    rows = sent.shape[1]
    depth = LINES // reps
    size = 2 * sent.size
    arrived, _ = pl.pallas_call(
        functools.partial(exchange_kernel, reps, tps),
        in_specs=[pl.BlockSpec(memory_space=pl.ANY)],
        out_specs=[pl.BlockSpec(memory_space=pl.ANY)] * 2,
        out_shape=[
            jax.ShapeDtypeStruct((tps, reps // tps, depth, rows, GROUP), jnp.bfloat16),
            jax.ShapeDtypeStruct((reps, depth, rows, GROUP), jnp.bfloat16),
        ],
        scratch_shapes=[pltpu.SemaphoreType.DMA((CHUNKS,))] * 4
        + [pltpu.SemaphoreType.DMA],
        compiler_params=pltpu.CompilerParams(collective_id=0, has_side_effects=True),
        cost_estimate=pl.CostEstimate(
            flops=0, bytes_accessed=60 * size, transcendentals=0
        ),
    )(sent)
    return arrived


def quantize_kernel(order, *refs):
    received, (scaled, scale) = refs[:-2], refs[-2:]
    group = pl.program_id(1)

    def run(ref):
        parts = [ref[where + (0,)] for where in order]
        served = jnp.concatenate(parts, axis=0).T.astype(jnp.float32)
        peak = jnp.max(jnp.abs(served), axis=0, keepdims=True) + 1e-06
        scaled[0] = (served * (1.0 / peak)).astype(jnp.bfloat16)
        scale[0, pl.ds(group, 1), :] = peak

    if len(received) == 1:
        run(received[0])
    else:
        for layer, ref in enumerate(received):
            pl.when(pl.program_id(0) == layer)(functools.partial(run, ref))


def quantize(received, order, groups, rows, places, earlier=()):
    total = len(order) * rows
    lead = received.shape[:-3]
    zeros = (0,) * len(lead)
    first, base = places[0]
    layers = len(places)
    return pl.pallas_call(
        lambda *refs: quantize_kernel(order, refs[0], refs[-2], refs[-1]),
        grid=(layers, groups),
        in_specs=[
            pl.BlockSpec(
                lead + (1, rows, GROUP), lambda l, g: zeros + (g, base + l, 0)
            )
        ]
        + [pl.BlockSpec(memory_space=pl.ANY)] * len(earlier),
        out_specs=[
            pl.BlockSpec((1, GROUP, total), lambda l, g: (first + l, g, 0)),
            pl.BlockSpec((1, groups, total), lambda l, g: (first + l, 0, 0)),
        ],
        out_shape=[
            jax.ShapeDtypeStruct((LAYERS, groups * GROUP, total), jnp.bfloat16),
            jax.ShapeDtypeStruct((LAYERS, groups, total), jnp.float32),
        ],
        input_output_aliases={1 + i: i for i in range(len(earlier))},
        cost_estimate=pl.CostEstimate(
            flops=20 * layers * groups * GROUP * total,
            bytes_accessed=4 * layers * groups * GROUP * total,
            transcendentals=0,
        ),
    )(received, *earlier)


def on_device(flat_buffer, shard_pad):
    reps = lax.axis_size("rep")
    tps = lax.axis_size("tp")
    devices = reps * tps
    ratio = reps // tps
    rows = [width // devices for width in WIDTHS]
    tiled = flat_buffer.reshape(flat_buffer.shape[0] // GROUP, GROUP)
    bases = np.concatenate([[0], np.cumsum(rows * LAYERS)[:-1]]) * LINES
    pads = shard_pad.reshape(-1)

    def starts(tensors, step):
        base, before = [], []
        for index, layer in tensors:
            place = layer * len(WIDTHS) + index
            for row in range(0, rows[index], step):
                base.append(bases[place] + row * LINES)
                before.append(np.arange(pads.shape[0]) < place)
        before = jnp.asarray(np.array(before))
        shifts = jnp.sum(jnp.where(before, pads[None, :], 0), axis=1)
        return shifts + jnp.asarray(np.array(base, np.int32))

    wide = math.gcd(rows[3], 96)
    step = math.gcd(*rows)
    sent_o = [prepare(tiled, starts([(3, layer)], wide), wide) for layer in range(LAYERS)]
    sent = prepare(tiled, starts(ORDER, step), step)

    def across(piece):
        got = lax.all_to_all(piece, "tp", split_axis=0, concat_axis=0, tiled=True)
        return got.reshape(tps, LINES // tps, rows[3], GROUP)

    early = across(sent_o[0])
    arrived = exchange(sent, reps, tps)
    arrived, late = lax.optimization_barrier((arrived, sent_o[1]))
    late = across(late)

    outputs = [()] * len(WIDTHS)
    order = [(where, part) for part in range(ratio) for where in range(tps)]
    begin = 0
    for index in (0, 1, 2, 4, 5):
        outputs[index] = quantize(
            arrived, order, LINES // reps, rows[index], [(0, begin // rows[index]), (1, 0)]
        )
        begin += LAYERS * rows[index]
    order = [(where,) for where in range(tps)]
    part = quantize(early, order, LINES // tps, rows[3], [(0, 0)])
    outputs[3] = quantize(late, order, LINES // tps, rows[3], [(1, 0)], tuple(part))
    return tuple(array for pair in outputs for array in pair)


def solution(mesh):
    column = P(None, "rep", "tp")
    row = P(None, "tp", "rep")
    return jax.shard_map(
        on_device,
        mesh=mesh,
        in_specs=(P(("rep", "tp")), P()),
        out_specs=(column,) * 6 + (row,) * 2 + (column,) * 4,
        check_vma=False,
    )
```

time: 1310 us -> 871 us (0.66)
  Pallas kernels: 77.7 us -> 832 us
  blocking collectives: 665 us -> 0 us
  waiting for transfers between devices: 396 us -> 0.01 us
  local copies, waits for them, and re-layouts: 79.5 us -> 13 us
  starting transfers between devices: 74.2 us -> 18.1 us
    pallas_call x12 -> x11, Pallas kernels: 77.7 us -> 832 us  [the longest x1 691 us: exchange(): pl.pallas_call(functools.partial(exchange_kernel, reps, tps), in_specs=[p...]
    all_to_all x9 -> x0, blocking collectives: 665 us -> none  [the longest x7 574 us: on_device(): lax.all_to_all(received, 'tp', split_axis=0, concat_axis=0, tiled=True)]
    all_to_all x13 -> x2, waiting for transfers between devices: 396 us -> 0.01 us  [across(): got = lax.all_to_all(piece, 'tp', split_axis=0, concat_axis=0, tiled=True)]
    all_to_all x13 -> x2, starting transfers between devices: 74.2 us -> 18.1 us  [across(): got = lax.all_to_all(piece, 'tp', split_axis=0, concat_axis=0, tiled=True)]
    transpose x12 -> x0, local copies, waits for them, and re-layouts: 39.5 us -> none  [on_device(): piece = taken.reshape(rows, lines, GROUP).transpose(1, 0, 2)]
    dynamic_slice x4 -> x0, local copies, waits for them, and re-layouts: 26.1 us -> none  [on_device(): lax.dynamic_slice_in_dim(tiled, offsets[layer * 6 + index], rows * lines, 0)]
  transfers between devices with their start and end apart: 13 -> 2, of which waited for: 13 -> 0; matrix products, arithmetic and copies ran while one was open for 5% -> 1% of each run, Pallas kernels for 5% -> 94%
where the time goes in v1:
time: 871 us; the launch traced here: 867 us
  Pallas kernels  832 us (96%)
  starting transfers between devices  18.1 us (2%)
  local copies, waits for them, and re-layouts  13 us (1%)
    pallas_call x1, Pallas kernels, exchange(): pl.pallas_call(functools.partial(exchange_kernel, reps, tps), in_specs=[p...  691 us
    pallas_call x7, Pallas kernels, quantize(): pl.pallas_call(lambda *refs: quantize_kernel(order, refs[0], refs[-2], re...  71.3 us
    pallas_call x3, Pallas kernels, prepare(): pl.pallas_call(prepare_kernel, grid_spec=pltpu.PrefetchScalarGridSpec(num...  69.6 us
    all_to_all x2, starting transfers between devices, across(): got = lax.all_to_all(piece, 'tp', split_axis=0, concat_axis=0, tiled=True)  18.1 us
  transfers between devices with their start and end apart: 2, of which 0 were waited for; matrix products, arithmetic and copies ran while one was open for 1% of the time, Pallas kernels for 94%

profile of v1, /device:TPU:1, one launch (start us, length us, event | category | flops | bytes accessed | tf_op | source)
XLA Modules:
  0.0 867.0 jit_solution(12723773984398995400)
XLA Ops:
  0.6 0.8 broadcast_in_dim.30
  1.4 0.8 select_reduce_fusion.1
  2.2 1.2 add.11.starts
  3.4 4.7 shard_map.181
  8.1 0.0 copy-start.2
  8.1 0.0 copy-start.4
  8.1 5.5 all-to-all-start.1
  13.6 0.0 copy-done.2
  13.6 0.1 select_reduce_fusion
  13.7 0.0 copy-done.4
  13.7 0.5 add.9.starts
  14.2 60.2 %shard_map.175.sent = bf16[48,2560,128]{2,1,0:T(8,128)(2,1)} custom-call(s32[80]{0:T(128)} %add.9.starts, bf16[141336,128]{1,0:T(8,128)(2,1)} %bitcast.4), custom_call_target="tpu_custom_call" | custom-call | flops 63242240 | bytes 63242240 | tf_op jit(solution)/shard_map/pallas_call | solution.py:36
  74.5 0.0 copy-start.3
  74.5 691.2 %shard_map.176 = (bf16[4,2,6,2560,128]{4,3,2,1,0:T(8,128)(2,1)}, bf16[8,6,2560,128]{3,2,1,0:T(8,128)(2,1)}) custom-call(bf16[48,2560,128]{2,1,0:T(8,128)(2,1)} %shard_map.175.sent), custom_call_target="tpu_custom_call" | custom-call | bytes 1887436800 | tf_op jit(solution)/shard_map/pallas_call | solution.py:168
  765.6 0.0 copy-done.3
  765.7 0.5 add.10.starts
  766.2 4.7 shard_map.177
  770.9 0.0 all-to-all-done.1
  770.9 0.0 copy-start.1
  770.9 1.4 copy-done.1
  772.3 12.5 %all-to-all-start = ((bf16[48,192,128]{2,1,0:T(8,128)(2,1)}), bf16[48,192,128]{2,1,0:T(8,128)(2,1)S(1)}, u32[]{:S(2)}, u32[]{:S(2)}) async-start(bf16[48,192,128]{2,1,0:T(8,128)(2,1)} %shard_map.177), calls=%async_computation | async-start | bytes 4718592 | tf_op jit(solution)/shard_map/all_to_all | solution.py:263
  784.9 9.5 %shard_map.178 = (bf16[2,768,1536]{2,1,0:T(8,128)(2,1)}, f32[2,6,1536]{2,1,0:T(8,128)}) custom-call(bf16[4,2,6,2560,128]{4,3,2,1,0:T(8,128)(2,1)} %get-tuple-element.30.refs_0_), custom_call_target="tpu_custom_call" | custom-call | flops 47185920 | bytes 9437184 | tf_op jit(solution)/shard_map/pallas_call | solution.py:210
  794.3 1.6 copy.28
  795.9 7.3 shard_map.179
  803.2 1.3 copy.29
  804.5 7.3 shard_map.180
  811.8 1.3 copy.30
  813.1 15.4 %shard_map.184 = (bf16[2,768,4096]{2,1,0:T(8,128)(2,1)}, f32[2,6,4096]{2,1,0:T(8,128)}) custom-call(bf16[4,2,6,2560,128]{4,3,2,1,0:T(8,128)(2,1)} %get-tuple-element.30.refs_0_), custom_call_target="tpu_custom_call" | custom-call | flops 125829120 | bytes 25165824 | tf_op jit(solution)/shard_map/pallas_call | solution.py:210
  828.5 1.8 copy.32
  830.3 15.4 %shard_map.185 = (bf16[2,768,4096]{2,1,0:T(8,128)(2,1)}, f32[2,6,4096]{2,1,0:T(8,128)}) custom-call(bf16[4,2,6,2560,128]{4,3,2,1,0:T(8,128)(2,1)} %get-tuple-element.30.refs_0_), custom_call_target="tpu_custom_call" | custom-call | flops 125829120 | bytes 25165824 | tf_op jit(solution)/shard_map/pallas_call | solution.py:210
  845.8 1.8 copy.33
  847.5 8.2 shard_map.182
  855.7 0.0 all-to-all-done
  855.7 0.0 copy-start
  855.7 1.4 copy-done
  857.2 8.2 shard_map.183
  865.4 1.6 copy.31
Async XLA Ops:
  8.1 5.5 copy-start.2
  8.1 5.6 copy-start.4
  8.1 762.8 %all-to-all-start.1 = ((bf16[48,192,128]{2,1,0:T(8,128)(2,1)}), bf16[48,192,128]{2,1,0:T(8,128)(2,1)S(1)}, u32[]{:S(2)}, u32[]{:S(2)}) async-start(bf16[48,192,128]{2,1,0:T(8,128)(2,1)} %shard_map.181), calls=%async_computation.1 | async-start | bytes 4718592 | tf_op jit(solution)/shard_map/all_to_all | solution.py:263
  74.5 691.2 %copy-start.3 = (s32[2]{0:T(128)S(1)}, s32[2]{0:T(128)}, u32[]{:S(2)}) copy-start(s32[2]{0:T(128)} %constant.17.clone) | copy-start | bytes 28
  770.9 1.4 copy-start.1
  772.3 83.4 %all-to-all-start = ((bf16[48,192,128]{2,1,0:T(8,128)(2,1)}), bf16[48,192,128]{2,1,0:T(8,128)(2,1)S(1)}, u32[]{:S(2)}, u32[]{:S(2)}) async-start(bf16[48,192,128]{2,1,0:T(8,128)(2,1)} %shard_map.177), calls=%async_computation | async-start | bytes 4718592 | tf_op jit(solution)/shard_map/all_to_all | solution.py:263
  855.7 1.4 copy-start

commit v2 on v1

--- a/solution.py
+++ b/solution.py
@@ -18,42 +18,61 @@
 LINES = D // GROUP
 ORDER = [(index, layer) for index in (0, 1, 2, 4, 5) for layer in range(LAYERS)]
 CHUNKS = 16
+PITCH = LINES + 4
 AHEAD = 2
 
 
-def prepare_kernel(starts, window, out, wide):
-    rows = out.shape[1]
-    shift = starts[pl.program_id(0)] % 8
-    wide[...] = window[...].astype(jnp.float32)
-    for line in range(LINES):
-        picked = wide[pl.ds(shift + line, rows, stride=LINES), :]
-        out[line] = picked.astype(jnp.bfloat16)
-
-
-def prepare(tiled, starts, rows):
-    steps = starts.shape[0]
+def prepare_kernel(pieces, starts, *refs):
+    windows, out, wide = refs[:pieces], refs[pieces], refs[pieces + 1]
+    rows = out.shape[1] // pieces
+    pitch = wide.shape[0] // (rows + 1)
+    for piece, window in enumerate(windows):
+        shift = starts[pl.program_id(0) * pieces + piece] % 8
+        for row in range(rows + 1):
+            count = min(LINES, window.shape[0] - row * LINES)
+            wide[pl.ds(row * pitch, count), :] = window[
+                pl.ds(row * LINES, count), :
+            ].astype(jnp.float32)
+        for line in range(LINES):
+            first = shift + line
+            first = jnp.where(first < LINES, first, first + pitch - LINES)
+            picked = wide[pl.ds(first, rows, stride=pitch), :]
+            out[line, pl.ds(piece * rows, rows)] = picked.astype(jnp.bfloat16)
+
+
+def prepare(tiled, starts, rows, pieces):
+    steps = starts.shape[0] // pieces
     span = rows * LINES + 8
+
+    def window(piece):
+        return pl.BlockSpec(
+            (pl.Element(span), pl.Element(GROUP)),
+            lambda i, starts: (
+                pl.multiple_of(starts[i * pieces + piece] // 8 * 8, 8),
+                0,
+            ),
+        )
+
     return pl.pallas_call(
-        prepare_kernel,
+        functools.partial(prepare_kernel, pieces),
         grid_spec=pltpu.PrefetchScalarGridSpec(
             num_scalar_prefetch=1,
             grid=(steps,),
-            in_specs=[
-                pl.BlockSpec(
-                    (pl.Element(span), pl.Element(GROUP)),
-                    lambda i, starts: (pl.multiple_of(starts[i] // 8 * 8, 8), 0),
-                )
-            ],
-            out_specs=pl.BlockSpec((LINES, rows, GROUP), lambda i, starts: (0, i, 0)),
-            scratch_shapes=[pltpu.VMEM((span, GROUP), jnp.float32)],
-        ),
-        out_shape=jax.ShapeDtypeStruct((LINES, steps * rows, GROUP), jnp.bfloat16),
+            in_specs=[window(piece) for piece in range(pieces)],
+            out_specs=pl.BlockSpec(
+                (LINES, pieces * rows, GROUP), lambda i, starts: (0, i, 0)
+            ),
+            scratch_shapes=[pltpu.VMEM(((rows + 1) * PITCH, GROUP), jnp.float32)],
+        ),
+        out_shape=jax.ShapeDtypeStruct(
+            (LINES, steps * pieces * rows, GROUP), jnp.bfloat16
+        ),
         cost_estimate=pl.CostEstimate(
-            flops=4 * steps * span * GROUP,
-            bytes_accessed=4 * steps * span * GROUP,
+            flops=4 * steps * pieces * span * GROUP,
+            bytes_accessed=4 * steps * pieces * span * GROUP,
             transcendentals=0,
         ),
-    )(starts, tiled)
+    )(starts, *[tiled] * pieces)
 
 
 def exchange_kernel(reps, tps, sent, arrived, passing, send_a, recv_a, send_b, recv_b, kept):
@@ -183,54 +202,89 @@
     return arrived
 
 
-def quantize_kernel(order, *refs):
-    received, (scaled, scale) = refs[:-2], refs[-2:]
-    group = pl.program_id(1)
-
-    def run(ref):
-        parts = [ref[where + (0,)] for where in order]
-        served = jnp.concatenate(parts, axis=0).T.astype(jnp.float32)
-        peak = jnp.max(jnp.abs(served), axis=0, keepdims=True) + 1e-06
-        scaled[0] = (served * (1.0 / peak)).astype(jnp.bfloat16)
-        scale[0, pl.ds(group, 1), :] = peak
-
-    if len(received) == 1:
-        run(received[0])
-    else:
-        for layer, ref in enumerate(received):
-            pl.when(pl.program_id(0) == layer)(functools.partial(run, ref))
-
-
-def quantize(received, order, groups, rows, places, earlier=()):
+def columns(order, rows):
+    width = math.gcd(rows, 256)
+    chunks, chunk, size = [], [], 0
+    for where in order:
+        for begin in range(0, rows, width):
+            chunk.append((where, begin, width))
+            size += width
+            if size % GROUP == 0 and size >= 256:
+                chunks.append(chunk)
+                chunk, size = [], 0
+    return chunks + [chunk] if chunk else chunks
+
+
+def quantize_kernel(chunks, members, first, *refs):
+    tensors = len(members)
+    received = refs[: sum(members)]
+    outputs = refs[-2 * tensors :]
+    taken = 0
+    for tensor in range(tensors):
+        scaled, scale = outputs[2 * tensor], outputs[2 * tensor + 1]
+        if first:
+            for before in range(first):
+                scale[:, before] = refs[-2 * tensors - 1][:, before]
+        for member in range(members[tensor]):
+            data = received[taken]
+            taken += 1
+            for group in range(scale.shape[0]):
+                column = 0
+                for chunk in chunks:
+                    parts = [
+                        data[where + (group, pl.ds(begin, width))]
+                        for where, begin, width in chunk
+                    ]
+                    part = parts[0] if len(parts) == 1 else jnp.concatenate(parts, axis=0)
+                    served = part.T.astype(jnp.float32)
+                    peak = jnp.max(jnp.abs(served), axis=0, keepdims=True) + 1e-06
+                    across = pl.ds(column, part.shape[0])
+                    scaled[member, pl.ds(group * GROUP, GROUP), across] = (
+                        served * (1.0 / peak)
+                    ).astype(jnp.bfloat16)
+                    scale[group, pl.ds(first + member, 1), across] = peak
+                    column += part.shape[0]
+
+
+def quantize(received, order, groups, rows, places, batch, first=0, earlier=()):
     total = len(order) * rows
     lead = received.shape[:-3]
     zeros = (0,) * len(lead)
-    first, base = places[0]
-    layers = len(places)
-    return pl.pallas_call(
-        lambda *refs: quantize_kernel(order, refs[0], refs[-2], refs[-1]),
-        grid=(layers, groups),
-        in_specs=[
+    members = [len(place) for place in places]
+    layers = members[0]
+    flat = [base for place in places for base in place]
+
+    def source(base):
+        return pl.BlockSpec(
+            lead + (batch, rows, GROUP), lambda g: zeros + (g, base, 0)
+        )
+
+    scale = pl.BlockSpec((batch, LAYERS, total), lambda g: (g, 0, 0))
+    outputs = pl.pallas_call(
+        functools.partial(quantize_kernel, columns(order, rows), members, first),
+        grid=(groups // batch,),
+        in_specs=[source(base) for base in flat]
+        + [pl.BlockSpec(memory_space=pl.ANY), scale][: len(earlier)],
+        out_specs=[
             pl.BlockSpec(
-                lead + (1, rows, GROUP), lambda l, g: zeros + (g, base + l, 0)
-            )
+                (layers, batch * GROUP, total), lambda g: (first // layers, g, 0)
+            ),
+            scale,
         ]
-        + [pl.BlockSpec(memory_space=pl.ANY)] * len(earlier),
-        out_specs=[
-            pl.BlockSpec((1, GROUP, total), lambda l, g: (first + l, g, 0)),
-            pl.BlockSpec((1, groups, total), lambda l, g: (first + l, 0, 0)),
-        ],
+        * len(places),
         out_shape=[
             jax.ShapeDtypeStruct((LAYERS, groups * GROUP, total), jnp.bfloat16),
-            jax.ShapeDtypeStruct((LAYERS, groups, total), jnp.float32),
-        ],
-        input_output_aliases={1 + i: i for i in range(len(earlier))},
+            jax.ShapeDtypeStruct((groups, LAYERS, total), jnp.float32),
+        ]
+        * len(places),
+        input_output_aliases={len(flat): 0} if earlier else {},
         cost_estimate=pl.CostEstimate(
-            flops=20 * layers * groups * GROUP * total,
-            bytes_accessed=4 * layers * groups * GROUP * total,
+            flops=20 * len(flat) * groups * GROUP * total,
+            bytes_accessed=4 * len(flat) * groups * GROUP * total,
             transcendentals=0,
         ),
-    )(received, *earlier)
+    )(*[received] * len(flat), *earlier)
+    return [tuple(outputs[2 * i : 2 * i + 2]) for i in range(len(places))]
 
 
 def on_device(flat_buffer, shard_pad):
@@ -255,9 +309,11 @@
         return shifts + jnp.asarray(np.array(base, np.int32))
 
     wide = math.gcd(rows[3], 96)
+    sent_o = [
+        prepare(tiled, starts([(3, layer)], wide), wide, 1) for layer in range(LAYERS)
+    ]
     step = math.gcd(*rows)
-    sent_o = [prepare(tiled, starts([(3, layer)], wide), wide) for layer in range(LAYERS)]
-    sent = prepare(tiled, starts(ORDER, step), step)
+    sent = prepare(tiled, starts(ORDER, step), step, math.gcd(rows[4] // step, 4))
 
     def across(piece):
         got = lax.all_to_all(piece, "tp", split_axis=0, concat_axis=0, tiled=True)
@@ -268,18 +324,36 @@
     arrived, late = lax.optimization_barrier((arrived, sent_o[1]))
     late = across(late)
 
-    outputs = [()] * len(WIDTHS)
+    begin, bases = 0, {}
+    for index, layer in ORDER:
+        bases[index, layer] = begin // rows[index]
+        begin += rows[index]
+    places = {
+        index: [bases[index, layer] for layer in range(LAYERS)]
+        for index in (0, 1, 2, 4, 5)
+    }
     order = [(where, part) for part in range(ratio) for where in range(tps)]
-    begin = 0
-    for index in (0, 1, 2, 4, 5):
-        outputs[index] = quantize(
-            arrived, order, LINES // reps, rows[index], [(0, begin // rows[index]), (1, 0)]
+    depth = LINES // reps
+    outputs = [None] * len(WIDTHS)
+    for batch, tensors in ((2, (4,)), (2, (5,)), (depth, (0,)), (depth, (1, 2))):
+        done = quantize(
+            arrived,
+            order,
+            depth,
+            rows[tensors[0]],
+            [places[index] for index in tensors],
+            math.gcd(batch, depth),
         )
-        begin += LAYERS * rows[index]
+        for index, pair in zip(tensors, done):
+            outputs[index] = pair
     order = [(where,) for where in range(tps)]
-    part = quantize(early, order, LINES // tps, rows[3], [(0, 0)])
-    outputs[3] = quantize(late, order, LINES // tps, rows[3], [(1, 0)], tuple(part))
-    return tuple(array for pair in outputs for array in pair)
+    depth = LINES // tps
+    batch = math.gcd(depth, 4)
+    part = quantize(early, order, depth, rows[3], [[0]], batch)[0]
+    outputs[3] = quantize(late, order, depth, rows[3], [[0]], batch, 1, part)[0]
+    return tuple(
+        array for scaled, scale in outputs for array in (scaled, scale.transpose(1, 0, 2))
+    )
 
 
 def solution(mesh):

time: 871 us -> 812 us (0.932)
  Pallas kernels: 832 us -> 773 us
  waiting for transfers between devices: 0.01 us -> 14.6 us
  local copies, waits for them, and re-layouts: 13 us -> 0.77 us
    pallas_call x10 -> x9, Pallas kernels: 141 us -> 82.1 us  [the longest x6 42.9 us: quantize(): pl.pallas_call(functools.partial(quantize_kernel, columns(order, rows), m...]
    all_to_all x2, waiting for transfers between devices: 0.01 us -> 14.6 us  [across(): got = lax.all_to_all(piece, 'tp', split_axis=0, concat_axis=0, tiled=True)]
    unnamed x16 -> x8, local copies, waits for them, and re-layouts: 12.2 us -> 0.01 us
  transfers between devices with their start and end apart: 2 -> 2, of which waited for: 0 -> 1; matrix products, arithmetic and copies ran while one was open for 1% -> 0% of each run, Pallas kernels for 94% -> 94%
where the time goes in v2:
time: 812 us; the launch traced here: 811 us
  Pallas kernels  773 us (95%)
  starting transfers between devices  18.1 us (2%)
  waiting for transfers between devices  14.6 us (2%)
    pallas_call x1, Pallas kernels, exchange(): pl.pallas_call(functools.partial(exchange_kernel, reps, tps), in_specs=[p...  691 us
    pallas_call x6, Pallas kernels, quantize(): pl.pallas_call(functools.partial(quantize_kernel, columns(order, rows), m...  42.9 us
    pallas_call x3, Pallas kernels, prepare(): pl.pallas_call(functools.partial(prepare_kernel, pieces), grid_spec=pltpu...  39.1 us
    all_to_all x2, starting transfers between devices, across(): got = lax.all_to_all(piece, 'tp', split_axis=0, concat_axis=0, tiled=True)  18.1 us
  transfers between devices with their start and end apart: 2, of which 1 were waited for; matrix products, arithmetic and copies ran while one was open for 0% of the time, Pallas kernels for 94%

profile of v2, /device:TPU:1, one launch (start us, length us, event | category | flops | bytes accessed | tf_op | source)
XLA Modules:
  0.0 810.5 jit_solution(16107811063037883766)
XLA Ops:
  0.6 0.8 broadcast_in_dim.30
  1.4 0.8 select_reduce_fusion.1
  2.2 1.2 add.11.starts
  3.4 3.7 shard_map.180
  7.1 0.0 copy-start.1
  7.1 0.0 copy-start.3
  7.1 5.5 all-to-all-start.1
  12.7 0.0 copy-done.1
  12.7 0.1 select_reduce_fusion
  12.8 0.0 copy-done.3
  12.8 0.5 add.9.starts
  13.3 31.6 %shard_map.175.sent = bf16[48,2560,128]{2,1,0:T(8,128)(2,1)} custom-call(s32[80]{0:T(128)} %add.9.starts, bf16[141336,128]{1,0:T(8,128)(2,1)} %bitcast.10, bf16[141336,128]{1,0:T(8,128)(2,1)} %bitcast.11, bf16[141336,128]{1,0:T(8,128)(2,1)} %bitcast.12, bf16[141336,128]{1,0:T(8,128)(2,1)} %bitcast.13), custom_call_target="tpu_custom_call" | custom-call | flops 63242240 | bytes 63242240 | tf_op jit(solution)/shard_map/pallas_call | solution.py:56
  44.9 0.0 copy-start.2
  44.9 691.2 %shard_map.176 = (bf16[4,2,6,2560,128]{4,3,2,1,0:T(8,128)(2,1)}, bf16[8,6,2560,128]{3,2,1,0:T(8,128)(2,1)}) custom-call(bf16[48,2560,128]{2,1,0:T(8,128)(2,1)} %shard_map.175.sent), custom_call_target="tpu_custom_call" | custom-call | bytes 1887436800 | tf_op jit(solution)/shard_map/pallas_call | solution.py:187
  736.1 0.0 copy-done.2
  736.1 0.5 add.10.starts
  736.6 3.8 shard_map.177
  740.4 0.0 all-to-all-done.1
  740.4 0.0 copy-start
  740.4 12.6 %all-to-all-start = ((bf16[48,192,128]{2,1,0:T(8,128)(2,1)}), bf16[48,192,128]{2,1,0:T(8,128)(2,1)}, u32[]{:S(2)}, u32[]{:S(2)}) async-start(bf16[48,192,128]{2,1,0:T(8,128)(2,1)} %shard_map.177), calls=%async_computation | async-start | bytes 4718592 | tf_op jit(solution)/shard_map/all_to_all | solution.py:319
  753.0 2.8 shard_map.179
  755.8 0.0 copy-done
  755.8 6.2 shard_map.178
  762.0 12.6 %shard_map.183 = (bf16[2,768,4096]{2,1,0:T(8,128)(2,1)}, f32[6,2,4096]{2,1,0:T(2,128)}) custom-call(bf16[4,2,6,2560,128]{4,3,2,1,0:T(8,128)(2,1)} %get-tuple-element.30.refs_0_.refs_1_.refs_2_.refs_3_, bf16[4,2,6,2560,128]{4,3,2,1,0:T(8,128)(2,1)} %get-tuple-element.30.refs_0_.refs_1_.refs_2_.refs_3_), custom_call_target="tpu_custom_call" | custom-call | flops 125829120 | bytes 25165824 | tf_op jit(solution)/shard_map/pallas_call | solution.py:263
  774.6 12.6 %shard_map.184 = (bf16[2,768,4096]{2,1,0:T(8,128)(2,1)}, f32[6,2,4096]{2,1,0:T(2,128)}) custom-call(bf16[4,2,6,2560,128]{4,3,2,1,0:T(8,128)(2,1)} %get-tuple-element.30.refs_0_.refs_1_.refs_2_.refs_3_, bf16[4,2,6,2560,128]{4,3,2,1,0:T(8,128)(2,1)} %get-tuple-element.30.refs_0_.refs_1_.refs_2_.refs_3_), custom_call_target="tpu_custom_call" | custom-call | flops 125829120 | bytes 25165824 | tf_op jit(solution)/shard_map/pallas_call | solution.py:263
  787.2 4.4 shard_map.181
  791.6 14.6 %all-to-all-done = bf16[48,192,128]{2,1,0:T(8,128)(2,1)} async-done(((bf16[48,192,128]{2,1,0:T(8,128)(2,1)}), bf16[48,192,128]{2,1,0:T(8,128)(2,1)}, u32[]{:S(2)}, u32[]{:S(2)}) %all-to-all-start) | async-done | bytes 2359328 | tf_op jit(solution)/shard_map/all_to_all | solution.py:319
  806.1 4.4 shard_map.182
Async XLA Ops:
  7.1 5.5 copy-start.1
  7.1 5.6 copy-start.3
  7.1 733.3 %all-to-all-start.1 = ((bf16[48,192,128]{2,1,0:T(8,128)(2,1)}), bf16[48,192,128]{2,1,0:T(8,128)(2,1)S(1)}, u32[]{:S(2)}, u32[]{:S(2)}) async-start(bf16[48,192,128]{2,1,0:T(8,128)(2,1)} %shard_map.180), calls=%async_computation.1 | async-start | bytes 4718592 | tf_op jit(solution)/shard_map/all_to_all | solution.py:319
  44.9 691.2 %copy-start.2 = (s32[2]{0:T(128)S(1)}, s32[2]{0:T(128)}, u32[]{:S(2)}) copy-start(s32[2]{0:T(128)} %constant.17.clone) | copy-start | bytes 28
  740.4 15.4 %copy-start = (bf16[48,192,128]{2,1,0:T(8,128)(2,1)}, bf16[48,192,128]{2,1,0:T(8,128)(2,1)S(1)}, u32[]{:S(2)}) copy-start(bf16[48,192,128]{2,1,0:T(8,128)(2,1)S(1)} %all-to-all-done.1) | copy-start | bytes 7077892
  740.4 65.7 %all-to-all-start = ((bf16[48,192,128]{2,1,0:T(8,128)(2,1)}), bf16[48,192,128]{2,1,0:T(8,128)(2,1)}, u32[]{:S(2)}, u32[]{:S(2)}) async-start(bf16[48,192,128]{2,1,0:T(8,128)(2,1)} %shard_map.177), calls=%async_computation | async-start | bytes 4718592 | tf_op jit(solution)/shard_map/all_to_all | solution.py:319

commit v3 on v2

--- a/solution.py
+++ b/solution.py
@@ -17,9 +17,9 @@
 WIDTHS = (D, KV, KV, D, FF, FF)
 LINES = D // GROUP
 ORDER = [(index, layer) for index in (0, 1, 2, 4, 5) for layer in range(LAYERS)]
-CHUNKS = 16
+CHUNKS = 32
 PITCH = LINES + 4
-AHEAD = 2
+AHEAD = 4
 
 
 def prepare_kernel(pieces, starts, *refs):
@@ -75,12 +75,66 @@
     )(starts, *[tiled] * pieces)
 
 
+def rotate_kernel(base, place, tps, pads, window, *refs):
+    outs, wide = refs[:-1], refs[-1]
+    depth, rows = outs[0].shape[:2]
+    pitch = wide.shape[0] // (rows + 1)
+    tp = lax.axis_index("tp")
+    shift = begin(base, place, pads) % 8
+    for row in range(rows + 1):
+        count = min(LINES, window.shape[0] - row * LINES)
+        wide[pl.ds(row * pitch, count), :] = window[pl.ds(row * LINES, count), :].astype(
+            jnp.float32
+        )
+    for hop, out in enumerate(outs):
+        for line in range(depth):
+            first = shift + (tp + hop) % tps * depth + line
+            first = jnp.where(first < LINES, first, first + pitch - LINES)
+            picked = wide[pl.ds(first, rows, stride=pitch), :]
+            out[line] = picked.astype(jnp.bfloat16)
+
+
+def begin(base, place, pads):
+    start = base
+    for earlier in range(place):
+        start = start + pads[earlier // len(WIDTHS), earlier % len(WIDTHS)]
+    return start
+
+
+def rotate(tiled, pads, base, place, rows, step, tps):
+    depth = LINES // tps
+    span = step * LINES + 8
+
+    def window(i, pads):
+        start = begin(base, place, pads) + i * step * LINES
+        return (pl.multiple_of(start // 8 * 8, 8), 0)
+
+    return pl.pallas_call(
+        functools.partial(rotate_kernel, base, place, tps),
+        grid_spec=pltpu.PrefetchScalarGridSpec(
+            num_scalar_prefetch=1,
+            grid=(rows // step,),
+            in_specs=[pl.BlockSpec((pl.Element(span), pl.Element(GROUP)), window)],
+            out_specs=[
+                pl.BlockSpec((depth, step, GROUP), lambda i, pads: (0, i, 0))
+            ]
+            * tps,
+            scratch_shapes=[pltpu.VMEM(((step + 1) * PITCH, GROUP), jnp.float32)],
+        ),
+        out_shape=[jax.ShapeDtypeStruct((depth, rows, GROUP), jnp.bfloat16)] * tps,
+        cost_estimate=pl.CostEstimate(
+            flops=4 * rows * D, bytes_accessed=4 * rows * D, transcendentals=0
+        ),
+    )(pads, tiled)
+
+
 def exchange_kernel(reps, tps, sent, arrived, passing, send_a, recv_a, send_b, recv_b, kept):
     rep = lax.axis_index("rep")
     tp = lax.axis_index("tp")
     ratio = reps // tps
     depth = LINES // reps
-    rows = sent.shape[1] // CHUNKS
+    chunks = math.gcd(sent.shape[1] // 8, CHUNKS)
+    rows = sent.shape[1] // chunks
     target = rep // ratio
 
     def at(device_rep, device_tp):
@@ -158,16 +212,16 @@
         whole = passing.at[pl.ds(0, count), :, block(chunk)]
         pltpu.make_async_copy(whole, whole, semaphore.at[chunk]).wait()
 
-    @pl.loop(0, CHUNKS)
+    @pl.loop(0, chunks)
     def _(chunk):
-        @pl.when(chunk + AHEAD < CHUNKS)
+        @pl.when(chunk + AHEAD < chunks)
         def _():
             spread(chunk + AHEAD)
 
         wait(recv_a, chunk, reps - 1)
         forward(chunk)
 
-    @pl.loop(0, CHUNKS)
+    @pl.loop(0, chunks)
     def _(chunk):
         wait(send_a, chunk, reps - 1)
         wait(send_b, chunk, ratio * (tps - 1))
@@ -215,43 +269,82 @@
     return chunks + [chunk] if chunk else chunks
 
 
-def quantize_kernel(chunks, members, first, *refs):
-    tensors = len(members)
-    received = refs[: sum(members)]
-    outputs = refs[-2 * tensors :]
-    taken = 0
-    for tensor in range(tensors):
+def settle(parts, scaled, scale, member, layer, group, column):
+    part = parts[0] if len(parts) == 1 else jnp.concatenate(parts, axis=0)
+    served = part.T.astype(jnp.float32)
+    peak = jnp.max(jnp.abs(served), axis=0, keepdims=True) + 1e-06
+    across = pl.ds(column, part.shape[0])
+    scaled[member, pl.ds(group * GROUP, GROUP), across] = (
+        served * (1.0 / peak)
+    ).astype(jnp.bfloat16)
+    scale[group, pl.ds(layer, 1), across] = peak
+    return column + part.shape[0]
+
+
+def quantize_kernel(chunks, *refs):
+    received, outputs = refs[: len(refs) // 2], refs[len(refs) // 2 :]
+    for which, data in enumerate(received):
+        tensor, layer = divmod(which, LAYERS)
         scaled, scale = outputs[2 * tensor], outputs[2 * tensor + 1]
-        if first:
-            for before in range(first):
-                scale[:, before] = refs[-2 * tensors - 1][:, before]
-        for member in range(members[tensor]):
-            data = received[taken]
-            taken += 1
-            for group in range(scale.shape[0]):
-                column = 0
-                for chunk in chunks:
-                    parts = [
-                        data[where + (group, pl.ds(begin, width))]
-                        for where, begin, width in chunk
-                    ]
-                    part = parts[0] if len(parts) == 1 else jnp.concatenate(parts, axis=0)
-                    served = part.T.astype(jnp.float32)
-                    peak = jnp.max(jnp.abs(served), axis=0, keepdims=True) + 1e-06
-                    across = pl.ds(column, part.shape[0])
-                    scaled[member, pl.ds(group * GROUP, GROUP), across] = (
-                        served * (1.0 / peak)
-                    ).astype(jnp.bfloat16)
-                    scale[group, pl.ds(first + member, 1), across] = peak
-                    column += part.shape[0]
-
-
-def quantize(received, order, groups, rows, places, batch, first=0, earlier=()):
+        for group in range(scale.shape[0]):
+            column = 0
+            for chunk in chunks:
+                parts = [
+                    data[where + (group, pl.ds(begin, width))]
+                    for where, begin, width in chunk
+                ]
+                column = settle(parts, scaled, scale, layer, layer, group, column)
+
+
+def finish_kernel(chunks, tps, layer, *refs):
+    received, scaled, scale = refs[:tps], refs[-2], refs[-1]
+    for before in range(layer):
+        scale[:, before] = refs[-3][:, before]
+
+    def run(mine):
+        for group in range(scale.shape[0]):
+            column = 0
+            for chunk in chunks:
+                parts = [
+                    received[(mine - where) % tps][group, pl.ds(begin, width)]
+                    for where, begin, width in chunk
+                ]
+                column = settle(parts, scaled, scale, 0, layer, group, column)
+
+    for mine in range(tps):
+        pl.when(lax.axis_index("tp") == mine)(functools.partial(run, mine))
+
+
+def finish(received, groups, rows, batch, layer, earlier=()):
+    tps = len(received)
+    total = tps * rows
+    scale = pl.BlockSpec((batch, LAYERS, total), lambda g: (g, 0, 0))
+    return pl.pallas_call(
+        functools.partial(finish_kernel, columns(range(tps), rows), tps, layer),
+        grid=(groups // batch,),
+        in_specs=[pl.BlockSpec((batch, rows, GROUP), lambda g: (g, 0, 0))] * tps
+        + [pl.BlockSpec(memory_space=pl.ANY), scale][: len(earlier)],
+        out_specs=[
+            pl.BlockSpec((1, batch * GROUP, total), lambda g: (layer, g, 0)),
+            scale,
+        ],
+        out_shape=[
+            jax.ShapeDtypeStruct((LAYERS, groups * GROUP, total), jnp.bfloat16),
+            jax.ShapeDtypeStruct((groups, LAYERS, total), jnp.float32),
+        ],
+        input_output_aliases={tps: 0} if earlier else {},
+        cost_estimate=pl.CostEstimate(
+            flops=20 * groups * GROUP * total,
+            bytes_accessed=4 * groups * GROUP * total,
+            transcendentals=0,
+        ),
+    )(*received, *earlier)
+
+
+def quantize(received, order, groups, rows, places, batch):
     total = len(order) * rows
     lead = received.shape[:-3]
     zeros = (0,) * len(lead)
-    members = [len(place) for place in places]
-    layers = members[0]
     flat = [base for place in places for base in place]
 
     def source(base):
@@ -259,17 +352,13 @@
             lead + (batch, rows, GROUP), lambda g: zeros + (g, base, 0)
         )
 
-    scale = pl.BlockSpec((batch, LAYERS, total), lambda g: (g, 0, 0))
     outputs = pl.pallas_call(
-        functools.partial(quantize_kernel, columns(order, rows), members, first),
+        functools.partial(quantize_kernel, columns(order, rows)),
         grid=(groups // batch,),
-        in_specs=[source(base) for base in flat]
-        + [pl.BlockSpec(memory_space=pl.ANY), scale][: len(earlier)],
+        in_specs=[source(base) for base in flat],
         out_specs=[
-            pl.BlockSpec(
-                (layers, batch * GROUP, total), lambda g: (first // layers, g, 0)
-            ),
-            scale,
+            pl.BlockSpec((LAYERS, batch * GROUP, total), lambda g: (0, g, 0)),
+            pl.BlockSpec((batch, LAYERS, total), lambda g: (g, 0, 0)),
         ]
         * len(places),
         out_shape=[
@@ -277,14 +366,13 @@
             jax.ShapeDtypeStruct((groups, LAYERS, total), jnp.float32),
         ]
         * len(places),
-        input_output_aliases={len(flat): 0} if earlier else {},
         cost_estimate=pl.CostEstimate(
             flops=20 * len(flat) * groups * GROUP * total,
             bytes_accessed=4 * len(flat) * groups * GROUP * total,
             transcendentals=0,
         ),
-    )(*[received] * len(flat), *earlier)
-    return [tuple(outputs[2 * i : 2 * i + 2]) for i in range(len(places))]
+    )(*[received] * len(flat))
+    return [outputs[2 * i : 2 * i + 2] for i in range(len(places))]
 
 
 def on_device(flat_buffer, shard_pad):
@@ -310,24 +398,32 @@
 
     wide = math.gcd(rows[3], 96)
     sent_o = [
-        prepare(tiled, starts([(3, layer)], wide), wide, 1) for layer in range(LAYERS)
+        rotate(tiled, shard_pad, int(bases[place]), place, rows[3], wide, tps)
+        for place in (3, 3 + len(WIDTHS))
     ]
+
+    def across(blocks):
+        hops = sorted(range(1, tps), key=lambda hop: abs(2 * hop - tps))
+        got = {
+            hop: lax.ppermute(
+                blocks[hop], "tp", [(at, (at + hop) % tps) for at in range(tps)]
+            )
+            for hop in hops
+        }
+        return [got.get(hop, blocks[0]) for hop in range(tps)]
+
+    early = across(sent_o[0])
     step = math.gcd(*rows)
     sent = prepare(tiled, starts(ORDER, step), step, math.gcd(rows[4] // step, 4))
-
-    def across(piece):
-        got = lax.all_to_all(piece, "tp", split_axis=0, concat_axis=0, tiled=True)
-        return got.reshape(tps, LINES // tps, rows[3], GROUP)
-
-    early = across(sent_o[0])
+    sent, late = lax.optimization_barrier((sent, sent_o[1]))
     arrived = exchange(sent, reps, tps)
-    arrived, late = lax.optimization_barrier((arrived, sent_o[1]))
+    arrived, late = lax.optimization_barrier((arrived, late))
     late = across(late)
 
-    begin, bases = 0, {}
+    begins, bases = 0, {}
     for index, layer in ORDER:
-        bases[index, layer] = begin // rows[index]
-        begin += rows[index]
+        bases[index, layer] = begins // rows[index]
+        begins += rows[index]
     places = {
         index: [bases[index, layer] for layer in range(LAYERS)]
         for index in (0, 1, 2, 4, 5)
@@ -346,11 +442,10 @@
         )
         for index, pair in zip(tensors, done):
             outputs[index] = pair
-    order = [(where,) for where in range(tps)]
     depth = LINES // tps
     batch = math.gcd(depth, 4)
-    part = quantize(early, order, depth, rows[3], [[0]], batch)[0]
-    outputs[3] = quantize(late, order, depth, rows[3], [[0]], batch, 1, part)[0]
+    part = finish(early, depth, rows[3], batch, 0)
+    outputs[3] = finish(late, depth, rows[3], batch, 1, tuple(part))
     return tuple(
         array for scaled, scale in outputs for array in (scaled, scale.transpose(1, 0, 2))
     )

time: 812 us -> 797 us (0.982); the launches traced: 811 us -> 786 us
  waiting for transfers between devices: 14.6 us -> 0.02 us
    all_to_all x2 -> x0, starting transfers between devices: 18.1 us -> none  [across(): got = lax.all_to_all(piece, 'tp', split_axis=0, concat_axis=0, tiled=True)]
    all_to_all x2 -> x0, waiting for transfers between devices: 14.6 us -> none  [across(): got = lax.all_to_all(piece, 'tp', split_axis=0, concat_axis=0, tiled=True)]
    ppermute x0 -> x6, starting transfers between devices: none -> 12.3 us  [across(): lax.ppermute(blocks[hop], 'tp', [(at, (at + hop) % tps) for at in range(t...]
    pallas_call x6 -> x8, Pallas kernels: 42.9 us -> 51.5 us  [the longest x4 34.2 us: quantize(): pl.pallas_call(functools.partial(quantize_kernel, columns(order, rows)),...]
    pallas_call x3 -> x1, Pallas kernels: 39.1 us -> 31.7 us  [prepare(): pl.pallas_call(functools.partial(prepare_kernel, pieces), grid_spec=pltpu...]
  transfers between devices with their start and end apart: 2 -> 6, of which waited for: 1 -> 0; matrix products, arithmetic and copies ran while one was open for 0% -> 0% of each run, Pallas kernels for 94% -> 97%
where the time goes in v3:
time: 797 us; the launch traced here: 786 us
  Pallas kernels  771 us (97%)
  starting transfers between devices  12.3 us (2%)
    pallas_call x1, Pallas kernels, exchange(): pl.pallas_call(functools.partial(exchange_kernel, reps, tps), in_specs=[p...  688 us
    pallas_call x4, Pallas kernels, quantize(): pl.pallas_call(functools.partial(quantize_kernel, columns(order, rows)),...  34.2 us
    pallas_call x1, Pallas kernels, prepare(): pl.pallas_call(functools.partial(prepare_kernel, pieces), grid_spec=pltpu...  31.7 us
  transfers between devices with their start and end apart: 6, of which 0 were waited for; matrix products, arithmetic and copies ran while one was open for 0% of the time, Pallas kernels for 97%

profile of v3, /device:TPU:1, one launch (start us, length us, event | category | flops | bytes accessed | tf_op | source)
XLA Modules:
  0.0 786.2 jit_solution(14567499125955396029)
XLA Ops:
  0.6 0.0 copy-start.4
  0.7 0.0 copy-start.5
  0.7 0.0 copy-start.8
  0.7 4.1 shard_map.144
  4.8 2.1 collective-permute-start.3
  6.9 2.3 collective-permute-start.4
  9.2 1.1 collective-permute-start.5
  10.3 0.0 copy-done.4
  10.3 0.1 broadcast_in_dim.14
  10.4 0.0 copy-done.5
  10.4 0.1 select_reduce_fusion
  10.5 0.0 copy-done.8
  10.5 0.5 add.3.starts
  11.0 31.7 %shard_map.139.sent = bf16[48,2560,128]{2,1,0:T(8,128)(2,1)} custom-call(s32[80]{0:T(128)} %add.3.starts, bf16[141336,128]{1,0:T(8,128)(2,1)} %bitcast.8, bf16[141336,128]{1,0:T(8,128)(2,1)} %bitcast.9, bf16[141336,128]{1,0:T(8,128)(2,1)} %bitcast.10, bf16[141336,128]{1,0:T(8,128)(2,1)} %bitcast.11), custom_call_target="tpu_custom_call" | custom-call | flops 63242240 | bytes 63242240 | tf_op jit(solution)/shard_map/pallas_call | solution.py:56
  42.7 4.0 shard_map.140
  46.7 0.0 copy-start.7
  46.7 0.0 copy-start.6
  46.7 688.0 %shard_map.141 = (bf16[4,2,6,2560,128]{4,3,2,1,0:T(8,128)(2,1)}, bf16[8,6,2560,128]{3,2,1,0:T(8,128)(2,1)}) custom-call(bf16[48,2560,128]{2,1,0:T(8,128)(2,1)} %shard_map.139.sent), custom_call_target="tpu_custom_call" | custom-call | bytes 1887436800 | tf_op jit(solution)/shard_map/pallas_call | solution.py:241
  734.7 4.6 collective-permute-start
  739.3 0.0 copy-done.7
  739.3 1.3 collective-permute-start.1
  740.6 0.0 collective-permute-done.3.refs_1_
  740.6 0.0 copy-done.6
  740.6 0.0 copy-start
  740.6 0.9 collective-permute-start.2
  741.6 2.8 shard_map.143
  744.4 0.0 copy-done
  744.4 6.2 shard_map.142
  750.5 12.6 %shard_map.147 = (bf16[2,768,4096]{2,1,0:T(8,128)(2,1)}, f32[6,2,4096]{2,1,0:T(2,128)}) custom-call(bf16[4,2,6,2560,128]{4,3,2,1,0:T(8,128)(2,1)} %get-tuple-element.55.refs_0_.refs_1_.refs_2_.refs_3_, bf16[4,2,6,2560,128]{4,3,2,1,0:T(8,128)(2,1)} %get-tuple-element.55.refs_0_.refs_1_.refs_2_.refs_3_), custom_call_target="tpu_custom_call" | custom-call | flops 125829120 | bytes 25165824 | tf_op jit(solution)/shard_map/pallas_call | solution.py:355
  763.1 12.6 %shard_map.148 = (bf16[2,768,4096]{2,1,0:T(8,128)(2,1)}, f32[6,2,4096]{2,1,0:T(2,128)}) custom-call(bf16[4,2,6,2560,128]{4,3,2,1,0:T(8,128)(2,1)} %get-tuple-element.55.refs_0_.refs_1_.refs_2_.refs_3_, bf16[4,2,6,2560,128]{4,3,2,1,0:T(8,128)(2,1)} %get-tuple-element.55.refs_0_.refs_1_.refs_2_.refs_3_), custom_call_target="tpu_custom_call" | custom-call | flops 125829120 | bytes 25165824 | tf_op jit(solution)/shard_map/pallas_call | solution.py:355
  775.7 0.0 collective-permute-done.4.refs_2_
  775.7 0.0 collective-permute-done.5.refs_3_
  775.7 4.6 shard_map.145
  780.3 0.0 collective-permute-done.refs_1_
  780.4 0.0 copy-start.1
  780.4 0.0 collective-permute-done.1.refs_2_
  780.4 0.0 copy-start.2
  780.4 0.0 collective-permute-done.2.refs_3_
  780.4 0.0 copy-start.3
  780.4 0.8 copy-done.1
  781.2 0.2 copy-done.2
  781.4 0.2 copy-done.3
  781.6 4.6 shard_map.146
Async XLA Ops:
  0.6 9.7 %copy-start.4 = (s32[2,6]{1,0:T(2,128)S(1)}, s32[2,6]{1,0:T(2,128)}, u32[]{:S(2)}) copy-start(s32[2,6]{1,0:T(2,128)} %pads.3) | copy-start | bytes 148
  0.7 9.7 %copy-start.5 = (pred[80,12]{0,1:T(8,128)(4,1)S(1)}, pred[80,12]{0,1:T(8,128)(4,1)}, u32[]{:S(2)}) copy-start(pred[80,12]{0,1:T(8,128)(4,1)} %constant.6.clone) | copy-start | bytes 2884
  0.7 9.8 %copy-start.8 = (s32[80]{0:T(128)S(1)}, s32[80]{0:T(128)}, u32[]{:S(2)}) copy-start(s32[80]{0:T(128)} %constant.7.clone) | copy-start | bytes 964
  4.8 735.8 %collective-permute-start.3 = (bf16[12,192,128]{2,1,0:T(8,128)(2,1)}, bf16[12,192,128]{2,1,0:T(8,128)(2,1)S(1)}, u32[]{:S(2)}, u32[]{:S(2)}) collective-permute-start(bf16[12,192,128]{2,1,0:T(8,128)(2,1)} %get-tuple-element.67), channel_id=1, source_target_pairs={{0,1},{1,2},{2,3},{3,0},{4,5},{5,6},{6,7},{7,4},{8,9},{9,10},{10,1... | collective-permute-start | bytes 1769480 | tf_op jit(solution)/shard_map/ppermute | solution.py:408
  6.9 768.8 %collective-permute-start.4 = (bf16[12,192,128]{2,1,0:T(8,128)(2,1)}, bf16[12,192,128]{2,1,0:T(8,128)(2,1)}, u32[]{:S(2)}, u32[]{:S(2)}) collective-permute-start(bf16[12,192,128]{2,1,0:T(8,128)(2,1)} %get-tuple-element.68), channel_id=1, source_target_pairs={{0,2},{1,3},{2,0},{3,1},{4,6},{5,7},{6,4},{7,5},{8,10},{9,11},{10,... | collective-permute-start | bytes 1769480 | tf_op jit(solution)/shard_map/ppermute | solution.py:408
  9.2 766.5 %collective-permute-start.5 = (bf16[12,192,128]{2,1,0:T(8,128)(2,1)}, bf16[12,192,128]{2,1,0:T(8,128)(2,1)}, u32[]{:S(2)}, u32[]{:S(2)}) collective-permute-start(bf16[12,192,128]{2,1,0:T(8,128)(2,1)} %get-tuple-element.69), channel_id=1, source_target_pairs={{0,3},{1,0},{2,1},{3,2},{4,7},{5,4},{6,5},{7,6},{8,11},{9,8},{10,9... | collective-permute-start | bytes 1769480 | tf_op jit(solution)/shard_map/ppermute | solution.py:408
  46.7 692.7 %copy-start.7 = (bf16[12,192,128]{2,1,0:T(8,128)(2,1)S(1)}, bf16[12,192,128]{2,1,0:T(8,128)(2,1)}, u32[]{:S(2)}) copy-start(bf16[12,192,128]{2,1,0:T(8,128)(2,1)} %get-tuple-element.64) | copy-start | bytes 1769476
  46.7 694.0 %copy-start.6 = (bf16[12,192,128]{2,1,0:T(8,128)(2,1)S(1)}, bf16[12,192,128]{2,1,0:T(8,128)(2,1)}, u32[]{:S(2)}) copy-start(bf16[12,192,128]{2,1,0:T(8,128)(2,1)} %get-tuple-element.65) | copy-start | bytes 1769476
  734.7 45.6 %collective-permute-start = (bf16[12,192,128]{2,1,0:T(8,128)(2,1)}, bf16[12,192,128]{2,1,0:T(8,128)(2,1)S(1)}, u32[]{:S(2)}, u32[]{:S(2)}) collective-permute-start(bf16[12,192,128]{2,1,0:T(8,128)(2,1)} %get-tuple-element.63), channel_id=1, source_target_pairs={{0,1},{1,2},{2,3},{3,0},{4,5},{5,6},{6,7},{7,4},{8,9},{9,10},{10,1... | collective-permute-start | bytes 1769480 | tf_op jit(solution)/shard_map/ppermute | solution.py:408
  739.3 41.0 %collective-permute-start.1 = (bf16[12,192,128]{2,1,0:T(8,128)(2,1)S(1)}, bf16[12,192,128]{2,1,0:T(8,128)(2,1)S(1)}, u32[]{:S(2)}, u32[]{:S(2)}) collective-permute-start(bf16[12,192,128]{2,1,0:T(8,128)(2,1)S(1)} %copy-done.7), channel_id=1, source_target_pairs={{0,2},{1,3},{2,0},{3,1},{4,6},{5,7},{6,4},{7,5},{8,10},{9,11},{10,... | collective-permute-start | bytes 1769480 | tf_op jit(solution)/shard_map/ppermute | solution.py:408
  740.6 3.8 copy-start
  740.6 39.8 %collective-permute-start.2 = (bf16[12,192,128]{2,1,0:T(8,128)(2,1)S(1)}, bf16[12,192,128]{2,1,0:T(8,128)(2,1)S(1)}, u32[]{:S(2)}, u32[]{:S(2)}) collective-permute-start(bf16[12,192,128]{2,1,0:T(8,128)(2,1)S(1)} %copy-done.6), channel_id=1, source_target_pairs={{0,3},{1,0},{2,1},{3,2},{4,7},{5,4},{6,5},{7,6},{8,11},{9,8},{10,9... | collective-permute-start | bytes 1769480 | tf_op jit(solution)/shard_map/ppermute | solution.py:408
  780.4 0.8 copy-start.1
  780.4 1.0 copy-start.2
  780.4 1.2 copy-start.3

commit v4 on v3

--- a/solution.py
+++ b/solution.py
@@ -20,6 +20,7 @@
 CHUNKS = 32
 PITCH = LINES + 4
 AHEAD = 4
+FIRST = 96
 
 
 def prepare_kernel(pieces, starts, *refs):
@@ -86,9 +87,11 @@
         wide[pl.ds(row * pitch, count), :] = window[pl.ds(row * LINES, count), :].astype(
             jnp.float32
         )
-    for hop, out in enumerate(outs):
+    halves = len(outs) // tps
+    for which, out in enumerate(outs):
+        hop, half = which // halves, which % halves
         for line in range(depth):
-            first = shift + (tp + hop) % tps * depth + line
+            first = shift + ((tp + hop) % tps * halves + half) * depth + line
             first = jnp.where(first < LINES, first, first + pitch - LINES)
             picked = wide[pl.ds(first, rows, stride=pitch), :]
             out[line] = picked.astype(jnp.bfloat16)
@@ -101,8 +104,8 @@
     return start
 
 
-def rotate(tiled, pads, base, place, rows, step, tps):
-    depth = LINES // tps
+def rotate(tiled, pads, base, place, rows, step, tps, halves):
+    depth = LINES // tps // halves
     span = step * LINES + 8
 
     def window(i, pads):
@@ -118,10 +121,13 @@
             out_specs=[
                 pl.BlockSpec((depth, step, GROUP), lambda i, pads: (0, i, 0))
             ]
-            * tps,
+            * tps
+            * halves,
             scratch_shapes=[pltpu.VMEM(((step + 1) * PITCH, GROUP), jnp.float32)],
         ),
-        out_shape=[jax.ShapeDtypeStruct((depth, rows, GROUP), jnp.bfloat16)] * tps,
+        out_shape=[jax.ShapeDtypeStruct((depth, rows, GROUP), jnp.bfloat16)]
+        * tps
+        * halves,
         cost_estimate=pl.CostEstimate(
             flops=4 * rows * D, bytes_accessed=4 * rows * D, transcendentals=0
         ),
@@ -269,70 +275,87 @@
     return chunks + [chunk] if chunk else chunks
 
 
-def settle(parts, scaled, scale, member, layer, group, column):
+def settle(parts, scaled, group, column):
     part = parts[0] if len(parts) == 1 else jnp.concatenate(parts, axis=0)
     served = part.T.astype(jnp.float32)
     peak = jnp.max(jnp.abs(served), axis=0, keepdims=True) + 1e-06
-    across = pl.ds(column, part.shape[0])
-    scaled[member, pl.ds(group * GROUP, GROUP), across] = (
+    scaled[0, pl.ds(group * GROUP, GROUP), pl.ds(column, part.shape[0])] = (
         served * (1.0 / peak)
     ).astype(jnp.bfloat16)
-    scale[group, pl.ds(layer, 1), across] = peak
-    return column + part.shape[0]
+    return peak
 
 
 def quantize_kernel(chunks, *refs):
-    received, outputs = refs[: len(refs) // 2], refs[len(refs) // 2 :]
-    for which, data in enumerate(received):
-        tensor, layer = divmod(which, LAYERS)
-        scaled, scale = outputs[2 * tensor], outputs[2 * tensor + 1]
+    tensors = len(refs) // 3
+    for tensor, data in enumerate(refs[:tensors]):
+        scaled, scale = refs[tensors + 2 * tensor :][:2]
         for group in range(scale.shape[0]):
-            column = 0
+            peaks, column = [], 0
             for chunk in chunks:
                 parts = [
                     data[where + (group, pl.ds(begin, width))]
                     for where, begin, width in chunk
                 ]
-                column = settle(parts, scaled, scale, layer, layer, group, column)
-
-
-def finish_kernel(chunks, tps, layer, *refs):
+                peaks.append(settle(parts, scaled, group, column))
+                column += peaks[-1].shape[1]
+            peaks = jnp.concatenate(peaks, axis=1)
+            for layer in range(LAYERS):
+
+                @pl.when(pl.program_id(1) == layer)
+                def _():
+                    scale[group, pl.ds(layer, 1), :] = peaks
+
+
+def finish_kernel(chunks, tps, layer, whole, *refs):
     received, scaled, scale = refs[:tps], refs[-2], refs[-1]
+    batch = scale.shape[0]
+    base = pl.program_id(0) * batch if whole else 0
     for before in range(layer):
         scale[:, before] = refs[-3][:, before]
 
     def run(mine):
-        for group in range(scale.shape[0]):
+        for group in range(batch):
             column = 0
             for chunk in chunks:
                 parts = [
-                    received[(mine - where) % tps][group, pl.ds(begin, width)]
+                    received[(mine - where) % tps][base + group, pl.ds(begin, width)]
                     for where, begin, width in chunk
                 ]
-                column = settle(parts, scaled, scale, 0, layer, group, column)
+                peak = settle(parts, scaled, group, column)
+                scale[group, pl.ds(layer, 1), pl.ds(column, peak.shape[1])] = peak
+                column += peak.shape[1]
 
     for mine in range(tps):
         pl.when(lax.axis_index("tp") == mine)(functools.partial(run, mine))
 
 
-def finish(received, groups, rows, batch, layer, earlier=()):
+def finish(received, depth, batch, layer, half=0, earlier=()):
     tps = len(received)
+    groups, rows = received[0].shape[:2]
     total = tps * rows
-    scale = pl.BlockSpec((batch, LAYERS, total), lambda g: (g, 0, 0))
+    skip = half * groups // batch
+    whole = layer > 0
+    if whole:
+        source = pl.BlockSpec(memory_space=pltpu.VMEM)
+    else:
+        source = pl.BlockSpec((batch, rows, GROUP), lambda g: (g, 0, 0))
+    scale = pl.BlockSpec((batch, LAYERS, total), lambda g: (skip + g, 0, 0))
     return pl.pallas_call(
-        functools.partial(finish_kernel, columns(range(tps), rows), tps, layer),
+        functools.partial(
+            finish_kernel, columns(range(tps), rows), tps, layer, whole
+        ),
         grid=(groups // batch,),
-        in_specs=[pl.BlockSpec((batch, rows, GROUP), lambda g: (g, 0, 0))] * tps
+        in_specs=[source] * tps
         + [pl.BlockSpec(memory_space=pl.ANY), scale][: len(earlier)],
         out_specs=[
-            pl.BlockSpec((1, batch * GROUP, total), lambda g: (layer, g, 0)),
+            pl.BlockSpec((1, batch * GROUP, total), lambda g: (layer, skip + g, 0)),
             scale,
         ],
         out_shape=[
-            jax.ShapeDtypeStruct((LAYERS, groups * GROUP, total), jnp.bfloat16),
-            jax.ShapeDtypeStruct((groups, LAYERS, total), jnp.float32),
+            jax.ShapeDtypeStruct((LAYERS, depth * GROUP, total), jnp.bfloat16),
+            jax.ShapeDtypeStruct((depth, LAYERS, total), jnp.float32),
         ],
-        input_output_aliases={tps: 0} if earlier else {},
+        input_output_aliases={tps: 0, tps + 1: 1} if earlier else {},
         cost_estimate=pl.CostEstimate(
             flops=20 * groups * GROUP * total,
             bytes_accessed=4 * groups * GROUP * total,
@@ -341,38 +364,37 @@
     )(*received, *earlier)
 
 
-def quantize(received, order, groups, rows, places, batch):
+def quantize(received, order, groups, rows, bases, batch):
     total = len(order) * rows
     lead = received.shape[:-3]
     zeros = (0,) * len(lead)
-    flat = [base for place in places for base in place]
 
     def source(base):
         return pl.BlockSpec(
-            lead + (batch, rows, GROUP), lambda g: zeros + (g, base, 0)
+            lead + (batch, rows, GROUP), lambda g, l: zeros + (g, base + l, 0)
         )
 
     outputs = pl.pallas_call(
         functools.partial(quantize_kernel, columns(order, rows)),
-        grid=(groups // batch,),
-        in_specs=[source(base) for base in flat],
+        grid=(groups // batch, LAYERS),
+        in_specs=[source(base) for base in bases],
         out_specs=[
-            pl.BlockSpec((LAYERS, batch * GROUP, total), lambda g: (0, g, 0)),
-            pl.BlockSpec((batch, LAYERS, total), lambda g: (g, 0, 0)),
+            pl.BlockSpec((1, batch * GROUP, total), lambda g, l: (l, g, 0)),
+            pl.BlockSpec((batch, LAYERS, total), lambda g, l: (g, 0, 0)),
         ]
-        * len(places),
+        * len(bases),
         out_shape=[
             jax.ShapeDtypeStruct((LAYERS, groups * GROUP, total), jnp.bfloat16),
             jax.ShapeDtypeStruct((groups, LAYERS, total), jnp.float32),
         ]
-        * len(places),
+        * len(bases),
         cost_estimate=pl.CostEstimate(
-            flops=20 * len(flat) * groups * GROUP * total,
-            bytes_accessed=4 * len(flat) * groups * GROUP * total,
+            flops=20 * len(bases) * LAYERS * groups * GROUP * total,
+            bytes_accessed=4 * len(bases) * LAYERS * groups * GROUP * total,
             transcendentals=0,
         ),
-    )(*[received] * len(flat))
-    return [outputs[2 * i : 2 * i + 2] for i in range(len(places))]
+    )(*[received] * len(bases))
+    return [outputs[2 * i : 2 * i + 2] for i in range(len(bases))]
 
 
 def on_device(flat_buffer, shard_pad):
@@ -396,10 +418,14 @@
         shifts = jnp.sum(jnp.where(before, pads[None, :], 0), axis=1)
         return shifts + jnp.asarray(np.array(base, np.int32))
 
-    wide = math.gcd(rows[3], 96)
+    wide = math.gcd(rows[3], FIRST)
+    halves = math.gcd(LINES // tps, 2)
     sent_o = [
-        rotate(tiled, shard_pad, int(bases[place]), place, rows[3], wide, tps)
-        for place in (3, 3 + len(WIDTHS))
+        rotate(
+            tiled, shard_pad, int(bases[3 + layer * len(WIDTHS)]),
+            3 + layer * len(WIDTHS), rows[3], wide, tps, halves if layer else 1,
+        )
+        for layer in range(LAYERS)
     ]
 
     def across(blocks):
@@ -418,20 +444,16 @@
     sent, late = lax.optimization_barrier((sent, sent_o[1]))
     arrived = exchange(sent, reps, tps)
     arrived, late = lax.optimization_barrier((arrived, late))
-    late = across(late)
-
-    begins, bases = 0, {}
-    for index, layer in ORDER:
-        bases[index, layer] = begins // rows[index]
-        begins += rows[index]
-    places = {
-        index: [bases[index, layer] for layer in range(LAYERS)]
-        for index in (0, 1, 2, 4, 5)
-    }
+    late = [across(late[half::halves]) for half in range(halves)]
+
+    place, places = 0, {}
+    for index in (0, 1, 2, 4, 5):
+        places[index] = place // rows[index]
+        place += LAYERS * rows[index]
     order = [(where, part) for part in range(ratio) for where in range(tps)]
     depth = LINES // reps
     outputs = [None] * len(WIDTHS)
-    for batch, tensors in ((2, (4,)), (2, (5,)), (depth, (0,)), (depth, (1, 2))):
+    for batch, tensors in ((3, (4,)), (3, (5,)), (3, (0,)), (depth, (1, 2))):
         done = quantize(
             arrived,
             order,
@@ -444,8 +466,10 @@
             outputs[index] = pair
     depth = LINES // tps
     batch = math.gcd(depth, 4)
-    part = finish(early, depth, rows[3], batch, 0)
-    outputs[3] = finish(late, depth, rows[3], batch, 1, tuple(part))
+    part = finish(early, depth, batch, 0)
+    for half in range(halves):
+        part = finish(late[half], depth, depth // halves, 1, half, tuple(part))
+    outputs[3] = part
     return tuple(
         array for scaled, scale in outputs for array in (scaled, scale.transpose(1, 0, 2))
     )

time: 797 us -> 801 us (level)
  transfers between devices with their start and end apart: 6 -> 9, of which waited for: 0 -> 1; matrix products, arithmetic and copies ran while one was open for 0% -> 0% of each run, Pallas kernels for 97% -> 96%
where the time goes in v4:
time: 801 us; the launch traced here: 798 us
  Pallas kernels  772 us (96%)
  starting transfers between devices  15.4 us (2%)
    pallas_call x1, Pallas kernels, exchange(): pl.pallas_call(functools.partial(exchange_kernel, reps, tps), in_specs=[p...  688 us
    pallas_call x4, Pallas kernels, quantize(): pl.pallas_call(functools.partial(quantize_kernel, columns(order, rows)),...  34.6 us
    pallas_call x1, Pallas kernels, prepare(): pl.pallas_call(functools.partial(prepare_kernel, pieces), grid_spec=pltpu...  31.7 us
  transfers between devices with their start and end apart: 9, of which 1 were waited for; matrix products, arithmetic and copies ran while one was open for 0% of the time, Pallas kernels for 96%

profile of v4, /device:TPU:1, one launch (start us, length us, event | category | flops | bytes accessed | tf_op | source)
XLA Modules:
  0.0 798.1 jit_solution(13744541416798959352)
XLA Ops:
  0.6 0.0 copy-start.9
  0.7 0.0 copy-start.10
  0.7 0.0 copy-start.12
  0.7 4.1 shard_map.144
  4.8 2.1 collective-permute-start.6
  6.9 2.3 collective-permute-start.7
  9.2 1.1 collective-permute-start.8
  10.3 0.0 copy-done.9
  10.3 0.1 broadcast_in_dim.14
  10.4 0.0 copy-done.10
  10.4 0.1 select_reduce_fusion
  10.5 0.0 copy-done.12
  10.5 0.5 add.3.starts
  11.0 4.0 shard_map.140
  15.0 31.7 %shard_map.139.sent = bf16[48,2560,128]{2,1,0:T(8,128)(2,1)} custom-call(s32[80]{0:T(128)} %add.3.starts, bf16[141336,128]{1,0:T(8,128)(2,1)} %bitcast.9, bf16[141336,128]{1,0:T(8,128)(2,1)} %bitcast.10, bf16[141336,128]{1,0:T(8,128)(2,1)} %bitcast.11, bf16[141336,128]{1,0:T(8,128)(2,1)} %bitcast.12), custom_call_target="tpu_custom_call" | custom-call | flops 63242240 | bytes 63242240 | tf_op jit(solution)/shard_map/pallas_call | solution.py:57
  46.7 0.0 copy-start.11
  46.7 688.0 %shard_map.141 = (bf16[4,2,6,2560,128]{4,3,2,1,0:T(8,128)(2,1)}, bf16[8,6,2560,128]{3,2,1,0:T(8,128)(2,1)}) custom-call(bf16[48,2560,128]{2,1,0:T(8,128)(2,1)} %shard_map.139.sent), custom_call_target="tpu_custom_call" | custom-call | bytes 1887436800 | tf_op jit(solution)/shard_map/pallas_call | solution.py:247
  734.6 0.0 copy-done.11
  734.7 4.6 collective-permute-start.3
  739.3 1.3 collective-permute-start.4
  740.6 7.1 collective-permute-done.3.refs_1_
  747.6 0.0 copy-start.4
  747.6 0.0 collective-permute-start.5
  747.6 0.0 collective-permute-done.6.refs_1_
  747.6 0.0 copy-start
  747.7 1.5 collective-permute-start
  749.1 0.0 collective-permute-done.7.refs_2_
  749.1 0.0 copy-start.1
  749.1 0.3 collective-permute-start.1
  749.4 0.0 collective-permute-done.8.refs_3_
  749.4 0.0 copy-start.2
  749.4 2.3 collective-permute-start.2
  751.7 4.4 shard_map.143
  756.1 0.0 copy-done.4
  756.2 0.0 copy-done
  756.2 0.0 copy-done.1
  756.2 0.0 copy-done.2
  756.2 6.2 shard_map.142
  762.4 12.0 %shard_map.148 = (bf16[2,768,4096]{2,1,0:T(8,128)(2,1)}, f32[6,2,4096]{2,1,0:T(2,128)}) custom-call(bf16[4,2,6,2560,128]{4,3,2,1,0:T(8,128)(2,1)} %get-tuple-element.77.refs_0_.refs_1_), custom_call_target="tpu_custom_call" | custom-call | flops 125829120 | bytes 25165824 | tf_op jit(solution)/shard_map/pallas_call | solution.py:377
  774.4 12.0 %shard_map.149 = (bf16[2,768,4096]{2,1,0:T(8,128)(2,1)}, f32[6,2,4096]{2,1,0:T(2,128)}) custom-call(bf16[4,2,6,2560,128]{4,3,2,1,0:T(8,128)(2,1)} %get-tuple-element.77.refs_0_.refs_1_), custom_call_target="tpu_custom_call" | custom-call | flops 125829120 | bytes 25165824 | tf_op jit(solution)/shard_map/pallas_call | solution.py:377
  786.3 4.6 shard_map.145
  790.9 0.0 collective-permute-done.4.refs_2_
  790.9 0.0 copy-start.5
  790.9 0.0 collective-permute-done.5.refs_3_
  790.9 0.0 copy-start.7
  790.9 0.7 copy-done.5
  791.6 0.1 copy-done.7
  791.7 2.7 shard_map.146
  794.5 0.0 collective-permute-done.refs_1_
  794.5 0.0 copy-start.3
  794.5 0.0 collective-permute-done.1.refs_2_
  794.5 0.0 copy-start.6
  794.5 0.0 collective-permute-done.2.refs_3_
  794.5 0.0 copy-start.8
  794.5 0.7 copy-done.3
  795.2 0.1 copy-done.6
  795.3 0.1 copy-done.8
  795.4 2.7 shard_map.147
Async XLA Ops:
  0.6 9.7 %copy-start.9 = (s32[2,6]{1,0:T(2,128)S(1)}, s32[2,6]{1,0:T(2,128)}, u32[]{:S(2)}) copy-start(s32[2,6]{1,0:T(2,128)} %pads.3) | copy-start | bytes 148
  0.7 9.7 %copy-start.10 = (pred[80,12]{0,1:T(8,128)(4,1)S(1)}, pred[80,12]{0,1:T(8,128)(4,1)}, u32[]{:S(2)}) copy-start(pred[80,12]{0,1:T(8,128)(4,1)} %constant.6.clone) | copy-start | bytes 2884
  0.7 9.8 %copy-start.12 = (s32[80]{0:T(128)S(1)}, s32[80]{0:T(128)}, u32[]{:S(2)}) copy-start(s32[80]{0:T(128)} %constant.7.clone) | copy-start | bytes 964
  4.8 742.8 %collective-permute-start.6 = (bf16[12,192,128]{2,1,0:T(8,128)(2,1)}, bf16[12,192,128]{2,1,0:T(8,128)(2,1)S(1)}, u32[]{:S(2)}, u32[]{:S(2)}) collective-permute-start(bf16[12,192,128]{2,1,0:T(8,128)(2,1)} %get-tuple-element.93), channel_id=1, source_target_pairs={{0,1},{1,2},{2,3},{3,0},{4,5},{5,6},{6,7},{7,4},{8,9},{9,10},{10,1... | collective-permute-start | bytes 1769480 | tf_op jit(solution)/shard_map/ppermute | solution.py:434
  6.9 742.2 %collective-permute-start.7 = (bf16[12,192,128]{2,1,0:T(8,128)(2,1)}, bf16[12,192,128]{2,1,0:T(8,128)(2,1)S(1)}, u32[]{:S(2)}, u32[]{:S(2)}) collective-permute-start(bf16[12,192,128]{2,1,0:T(8,128)(2,1)} %get-tuple-element.94), channel_id=1, source_target_pairs={{0,2},{1,3},{2,0},{3,1},{4,6},{5,7},{6,4},{7,5},{8,10},{9,11},{10,... | collective-permute-start | bytes 1769480 | tf_op jit(solution)/shard_map/ppermute | solution.py:434
  9.2 740.2 %collective-permute-start.8 = (bf16[12,192,128]{2,1,0:T(8,128)(2,1)}, bf16[12,192,128]{2,1,0:T(8,128)(2,1)S(1)}, u32[]{:S(2)}, u32[]{:S(2)}) collective-permute-start(bf16[12,192,128]{2,1,0:T(8,128)(2,1)} %get-tuple-element.95), channel_id=1, source_target_pairs={{0,3},{1,0},{2,1},{3,2},{4,7},{5,4},{6,5},{7,6},{8,11},{9,8},{10,9... | collective-permute-start | bytes 1769480 | tf_op jit(solution)/shard_map/ppermute | solution.py:434
  46.7 688.0 %copy-start.11 = (bf16[6,192,128]{2,1,0:T(8,128)(2,1)S(1)}, bf16[6,192,128]{2,1,0:T(8,128)(2,1)}, u32[]{:S(2)}) copy-start(bf16[6,192,128]{2,1,0:T(8,128)(2,1)} %get-tuple-element.89) | copy-start | bytes 884740
  734.7 13.0 %collective-permute-start.3 = (bf16[6,192,128]{2,1,0:T(8,128)(2,1)S(1)}, bf16[6,192,128]{2,1,0:T(8,128)(2,1)S(1)}, u32[]{:S(2)}, u32[]{:S(2)}) collective-permute-start(bf16[6,192,128]{2,1,0:T(8,128)(2,1)S(1)} %copy-done.11), channel_id=1, source_target_pairs={{0,1},{1,2},{2,3},{3,0},{4,5},{5,6},{6,7},{7,4},{8,9},{9,10},{10,1... | collective-permute-start | bytes 884744 | tf_op jit(solution)/shard_map/ppermute | solution.py:434
  739.3 51.7 %collective-permute-start.4 = (bf16[6,192,128]{2,1,0:T(8,128)(2,1)}, bf16[6,192,128]{2,1,0:T(8,128)(2,1)S(1)}, u32[]{:S(2)}, u32[]{:S(2)}) collective-permute-start(bf16[6,192,128]{2,1,0:T(8,128)(2,1)} %get-tuple-element.90), channel_id=1, source_target_pairs={{0,2},{1,3},{2,0},{3,1},{4,6},{5,7},{6,4},{7,5},{8,10},{9,11},{10,... | collective-permute-start | bytes 884744 | tf_op jit(solution)/shard_map/ppermute | solution.py:434
  747.6 8.5 %copy-start.4 = (bf16[6,192,128]{2,1,0:T(8,128)(2,1)}, bf16[6,192,128]{2,1,0:T(8,128)(2,1)S(1)}, u32[]{:S(2)}) copy-start(bf16[6,192,128]{2,1,0:T(8,128)(2,1)S(1)} %collective-permute-done.3.refs_1_) | copy-start | bytes 884740
  747.6 43.3 %collective-permute-start.5 = (bf16[6,192,128]{2,1,0:T(8,128)(2,1)}, bf16[6,192,128]{2,1,0:T(8,128)(2,1)S(1)}, u32[]{:S(2)}, u32[]{:S(2)}) collective-permute-start(bf16[6,192,128]{2,1,0:T(8,128)(2,1)} %get-tuple-element.91), channel_id=1, source_target_pairs={{0,3},{1,0},{2,1},{3,2},{4,7},{5,4},{6,5},{7,6},{8,11},{9,8},{10,9... | collective-permute-start | bytes 884744 | tf_op jit(solution)/shard_map/ppermute | solution.py:434
  747.6 8.5 %copy-start = (bf16[12,192,128]{2,1,0:T(8,128)(2,1)}, bf16[12,192,128]{2,1,0:T(8,128)(2,1)S(1)}, u32[]{:S(2)}) copy-start(bf16[12,192,128]{2,1,0:T(8,128)(2,1)S(1)} %collective-permute-done.6.refs_1_) | copy-start | bytes 1769476
  747.7 46.8 %collective-permute-start = (bf16[6,192,128]{2,1,0:T(8,128)(2,1)}, bf16[6,192,128]{2,1,0:T(8,128)(2,1)S(1)}, u32[]{:S(2)}, u32[]{:S(2)}) collective-permute-start(bf16[6,192,128]{2,1,0:T(8,128)(2,1)} %get-tuple-element.85), channel_id=1, source_target_pairs={{0,1},{1,2},{2,3},{3,0},{4,5},{5,6},{6,7},{7,4},{8,9},{9,10},{10,1... | collective-permute-start | bytes 884744 | tf_op jit(solution)/shard_map/ppermute | solution.py:434
  749.1 7.0 copy-start.1
  749.1 45.3 %collective-permute-start.1 = (bf16[6,192,128]{2,1,0:T(8,128)(2,1)}, bf16[6,192,128]{2,1,0:T(8,128)(2,1)S(1)}, u32[]{:S(2)}, u32[]{:S(2)}) collective-permute-start(bf16[6,192,128]{2,1,0:T(8,128)(2,1)} %get-tuple-element.86), channel_id=1, source_target_pairs={{0,2},{1,3},{2,0},{3,1},{4,6},{5,7},{6,4},{7,5},{8,10},{9,11},{10,... | collective-permute-start | bytes 884744 | tf_op jit(solution)/shard_map/ppermute | solution.py:434
  749.4 6.7 copy-start.2
  749.4 45.1 %collective-permute-start.2 = (bf16[6,192,128]{2,1,0:T(8,128)(2,1)}, bf16[6,192,128]{2,1,0:T(8,128)(2,1)S(1)}, u32[]{:S(2)}, u32[]{:S(2)}) collective-permute-start(bf16[6,192,128]{2,1,0:T(8,128)(2,1)} %get-tuple-element.87), channel_id=1, source_target_pairs={{0,3},{1,0},{2,1},{3,2},{4,7},{5,4},{6,5},{7,6},{8,11},{9,8},{10,9... | collective-permute-start | bytes 884744 | tf_op jit(solution)/shard_map/ppermute | solution.py:434
  790.9 0.7 copy-start.5
  790.9 0.8 copy-start.7
  794.5 0.7 copy-start.3
  794.5 0.8 copy-start.6
  794.5 0.9 copy-start.8
